TPU v7x, 32 devices: a whole 2x2x4 slice. The times are simulated.
32 devices in a mesh: gx: 16 (over z, y, x), gz: 2 (over core).
Axes of the slice: x: 2, y: 2, z: 4, core: 2. Of those that a mesh axis runs over, the one named last changes fastest.
Arguments:
- state: float32 [5, 128, 16, 256], P(None, 'gx', None, 'gz'), may hold values from -1 to 8.5, as said below
- register: float32 [5, 128, 16, 256], P(None, 'gx', None, 'gz'), may hold values from -2.4 to 2.4
- top_ghost: float32 [5, 128, 3, 256], P(None, 'gx', None, 'gz'), may hold values from -1 to 8.5, as said below
- flags: int32 [128, 16, 2], P('gx', None, 'gz'), may hold values 0 or 1
Outputs:
- new_state: float32 [5, 128, 16, 256], P(None, 'gx', None, 'gz')
- new_register: float32 [5, 128, 16, 256], P(None, 'gx', None, 'gz')
Inputs may be any that keep to these rules, and one draw needn't show every extreme that they name: `state`: conserved variables of an ideal gas with ratio of heats 1.4, density 0.5 to 2 and pressure 0.3 to 1.5 in every cell. `top_ghost`: conserved variables of an ideal gas with ratio of heats 1.4, density 0.5 to 2 and pressure 0.3 to 1.5 in every cell.
All inputs are finite; a program needn't handle non-finite values. No bound on the sum of `flags` on one device may be relied on, other than what follows from the above.
Results may differ from a plain program's by a relative error of at most 0.0003.
Values sent between devices are 32-bit elements; how exact they have to be, the bound alone decides.
A program may use at most 64 MiB of HBM per device.

v0:
```python
import functools

import jax
import jax.numpy as jnp
from jax import lax
from jax.experimental import pallas as pl
from jax.experimental.pallas import tpu as pltpu
from jax.sharding import PartitionSpec as P

MESH = pl.DeviceIdType.MESH
GAMMA = 1.4
EPS_WENO = 1e-06
LAMBDA = (0.1, 0.15, 0.1)
REGISTER_DECAY = -5.0 / 9.0
UPDATE_WEIGHT = 15.0 / 16.0
UNROLL_LIMIT = 64


def reciprocal(value):
    guess = pl.reciprocal(value, approx=True)
    return guess * (2.0 - value * guess)


def pressure_velocity(cons):
    inverse = reciprocal(cons[0])
    vel = [cons[1] * inverse, cons[2] * inverse, cons[3] * inverse]
    pressure = (GAMMA - 1.0) * (
        cons[4] - 0.5 * (cons[1] * vel[0] + cons[2] * vel[1] + cons[3] * vel[2])
    )
    return inverse, vel, pressure


def shifted(me, step, count):
    moved = me + step
    return jnp.where(moved >= count, moved - count, moved)


def exchange_peers(gx, gz, ngx, ngz):
    offsets = [(dx, dz) for dx in range(ngx) for dz in range(ngz)][1:]

    def each_peer(action):
        if len(offsets) < UNROLL_LIMIT:
            for slot, (dx, dz) in enumerate(offsets):
                action(slot, shifted(gx, dx, ngx), shifted(gz, dz, ngz))
        else:
            def body(slot, carry):
                dx, dz = (slot + 1) // ngz, (slot + 1) % ngz
                action(slot, shifted(gx, dx, ngx), shifted(gz, dz, ngz))
                return carry
            lax.fori_loop(0, len(offsets), body, 0)

    return each_peer, len(offsets)


class Line:
    def __init__(self, load):
        cached = functools.lru_cache(None)
        self.load = cached(load)
        self.D = cached(lambda j: self.load(j + 1) - self.load(j))
        self.S = cached(lambda j: self.D(j) - self.D(j - 1))
        self.T = cached(lambda j: self.S(j + 1) - self.S(j))
        self.S2 = cached(lambda j: self.S(j) + self.S(j))
        self.C = cached(
            lambda j: (self.S(j) * self.S(j) * (4.0 / 3.0) + 4.0 * EPS_WENO)
            + self.D(j) * self.D(j - 1)
        )

    def L(self, j):
        return self.C(j) + self.S2(j) * self.D(j)

    def R(self, j):
        return self.C(j) - self.S2(j) * self.D(j - 1)


def correction(near, mid, far, t_near, t_far):
    a, b, c = mid * far, near * far, near * mid
    w_near = a * a
    w_far = 3.0 * (c * c)
    total = w_near + 6.0 * (b * b) + w_far
    return (w_far * t_far + (w_near + w_near) * t_near) * reciprocal(total)


def line_divergence(count, alpha, load_flux, load_cons, emit):
    flux = functools.lru_cache(None)(load_flux)
    drift = functools.lru_cache(None)(lambda j: alpha * load_cons(j))
    plus, minus = Line(lambda j: flux(j) + drift(j)), Line(lambda j: flux(j) - drift(j))

    def face(j):
        up = correction(plus.L(j - 1), plus.C(j), plus.R(j + 1), plus.T(j - 1), plus.T(j))
        down = correction(minus.R(j + 2), minus.C(j + 1), minus.L(j), minus.T(j + 1), minus.T(j))
        return 6.0 * (flux(j) + flux(j + 1)) - (plus.S(j) + minus.S(j + 1)) - up + down

    before = face(2)
    for cell in range(count):
        j = cell + 3
        after = face(j)
        central = (
            9.0 * (flux(j + 1) - flux(j - 1))
            - 1.8 * (flux(j + 2) - flux(j - 2))
            + 0.2 * (flux(j + 3) - flux(j - 3))
        )
        emit(cell, after - before, central)
        before = after


def store_fluxes(cons, var, fluxes, conserved, cell):
    _, vel, pressure = pressure_velocity(cons)
    velocity = vel[var - 1]
    for field in range(5):
        if field == 4:
            flux = (cons[4] + pressure) * velocity
        else:
            flux = cons[field] * velocity
        if field == var:
            flux = flux + pressure
        fluxes[field, cell] = flux
        conserved[field, cell] = cons[field]


def step_kernel(
    ngx, ngz, cx, ny, state_ref, ghost_ref, flags_ref, acc, xpad, zt, ghost, flags,
    slots, mine, mask, acc_t, zf, zu, yf, yu, xf, xu,
    load_sem, side_sem, send_sem, recv_sem, halo_send, halo_recv, out_sem
):
    gx, gz = lax.axis_index("gx"), lax.axis_index("gz")
    rows = cx * ny
    halo = 3 * ny
    strip = zt.shape[1] - 16
    chunk = strip // 8
    load = pltpu.make_async_copy(state_ref, xpad.at[:, pl.ds(halo, rows), :], load_sem)
    load.start()
    load_flags = pltpu.make_async_copy(flags_ref, flags, side_sem.at[0])
    load_flags.start()
    load_ghost = pltpu.make_async_copy(ghost_ref, ghost, side_sem.at[1])
    load_ghost.start()
    barrier = pltpu.get_barrier_semaphore()
    each_peer, peers = exchange_peers(gx, gz, ngx, ngz)

    def greet(slot, tx, tz):
        pl.semaphore_signal(barrier, inc=1, device_id=(tx, tz), device_id_type=MESH)

    each_peer(greet)
    load.wait()
    best = None
    for row in range(0, rows, 8):
        cons = [xpad[var, pl.ds(halo + row, 8), :] for var in range(5)]
        inverse, vel, pressure = pressure_velocity(cons)
        sound = jnp.sqrt(GAMMA * pressure * inverse)
        local = [jnp.abs(v) + sound for v in vel]
        best = local if best is None else [jnp.maximum(a, b) for a, b in zip(best, local)]
    tops = [jnp.max(jnp.max(b, axis=0, keepdims=True), axis=1, keepdims=True) for b in best]
    lane = lax.broadcasted_iota(jnp.int32, (1, 128), 1)
    mine[...] = jnp.where(lane == 0, tops[0], jnp.where(lane == 1, tops[1], tops[2]))

    pl.semaphore_wait(barrier, peers)

    def send(slot, tx, tz):
        pltpu.make_async_remote_copy(
            src_ref=mine, dst_ref=slots.at[slot], send_sem=send_sem, recv_sem=recv_sem,
            device_id=(tx, tz), device_id_type=MESH,
        ).start()

    each_peer(send)
    right, left = shifted(gx, 1, ngx), shifted(gx, ngx - 1, ngx)
    high, low = shifted(gz, 1, ngz), shifted(gz, ngz - 1, ngz)

    def move(index, src, dst, target):
        copy = pltpu.make_async_remote_copy(
            src_ref=src, dst_ref=dst, send_sem=halo_send.at[index], recv_sem=halo_recv.at[index],
            device_id=target, device_id_type=MESH,
        )
        copy.start()
        return copy

    x_copies = [
        move(0, xpad.at[:, pl.ds(halo, halo), :], xpad.at[:, pl.ds(halo + rows, halo), :], (left, gz)),
        move(1, xpad.at[:, pl.ds(rows, halo), :], xpad.at[:, pl.ds(0, halo), :], (right, gz)),
    ]
    for var in range(5):
        zt[var, pl.ds(8, strip), :] = xpad[var, pl.ds(halo, rows), :].T
    load_flags.wait()
    for x in range(cx):
        wide = jnp.broadcast_to(flags[x], (strip, ny)).astype(jnp.float32)
        mask[pl.ds(x * ny, ny), :] = wide.T
    z_copies = [
        move(2, zt.at[:, pl.ds(8, 8), :], zt.at[:, pl.ds(8 + strip, 8), :], (gx, low)),
        move(3, zt.at[:, pl.ds(strip, 8), :], zt.at[:, pl.ds(0, 8), :], (gx, high)),
    ]
    flag_t = mask[...].T[:8] > 0.0

    load_ghost.wait()
    for cell in range(ny + 6):
        y = cell - 3
        if y < ny:
            source = y if y >= 0 else -1 - y
            cons = [xpad[f, pl.ds(halo + source, 8, stride=ny), :] for f in range(5)]
            if y < 0:
                cons[2] = -cons[2]
        else:
            cons = [ghost[f, y - ny] for f in range(5)]
        store_fluxes(cons, 2, yf, yu, cell)

    for copy in z_copies:
        copy.wait()
    for cell in range(chunk + 6):
        cons = [zt[f, pl.ds(5 + cell, 8, stride=chunk), :] for f in range(5)]
        store_fluxes(cons, 3, zf, zu, cell)

    pltpu.make_async_copy(slots, slots, recv_sem).wait()
    top = jnp.maximum(jnp.max(slots[...], axis=0), mine[...])
    alpha = [jnp.broadcast_to(top[:, k : k + 1], (8, 128)) for k in range(3)]

    def z_field(f, carry):
        def emit(cell, upwind, central):
            acc_t[f, pl.ds(cell, 8, stride=chunk), :] = (LAMBDA[2] / 12.0) * jnp.where(
                flag_t, upwind, central
            )
        line_divergence(chunk, alpha[2], lambda j: zf[f, j], lambda j: zu[f, j], emit)
        return carry

    lax.fori_loop(0, 5, z_field, 0)
    for f in range(5):
        acc[f] = acc_t[f].T

    def y_field(f, carry):
        def emit(cell, upwind, central):
            where = pl.ds(cell, 8, stride=ny)
            acc[f, where, :] = acc[f, where, :] + (LAMBDA[1] / 12.0) * jnp.where(
                mask[where, :] > 0.0, upwind, central
            )
        line_divergence(ny, alpha[1], lambda j: yf[f, j], lambda j: yu[f, j], emit)
        return carry

    lax.fori_loop(0, 5, y_field, 0)

    for copy in x_copies:
        copy.wait()
    for part in range(ny // 8):
        for cell in range(cx + 6):
            cons = [xpad[f, pl.ds(cell * ny + part * 8, 8), :] for f in range(5)]
            store_fluxes(cons, 1, xf.at[part], xu.at[part], cell)

    def x_field(f, carry):
        for part in range(ny // 8):
            def emit(cell, upwind, central):
                where = pl.ds(cell * ny + part * 8, 8)
                acc[f, where, :] = acc[f, where, :] + (LAMBDA[0] / 12.0) * jnp.where(
                    mask[where, :] > 0.0, upwind, central
                )
            line_divergence(
                cx, alpha[0], lambda j: xf[part, f, j], lambda j: xu[part, f, j], emit
            )
        return carry

    lax.fori_loop(0, 5, x_field, 0)
    pltpu.make_async_copy(slots, slots, send_sem).wait()


def shards(ngx, ngz, state, register, top_ghost, flags):
    _, cx, ny, cz = state.shape
    rows = cx * ny
    peers = ngx * ngz - 1
    f32 = jnp.float32
    anywhere = pl.BlockSpec(memory_space=pl.ANY)
    flat = state.reshape(5, rows, cz)
    change = pl.pallas_call(
        functools.partial(step_kernel, ngx, ngz, cx, ny),
        out_shape=pltpu.VMEM((5, rows, cz), f32),
        in_specs=[anywhere] * 3,
        out_specs=pl.BlockSpec(memory_space=pltpu.VMEM),
        scratch_shapes=[
            pltpu.VMEM((5, (cx + 6) * ny, cz), f32),
            pltpu.VMEM((5, cz + 16, rows), f32),
            pltpu.VMEM((5, 3, cx, cz), f32),
            pltpu.VMEM((cx, 1, ny), jnp.int32),
            pltpu.VMEM((peers, 1, 128), f32),
            pltpu.VMEM((1, 128), f32),
            pltpu.VMEM((rows, cz), f32),
            pltpu.VMEM((5, cz, rows), f32),
            pltpu.VMEM((5, cz // 8 + 6, 8, rows), f32),
            pltpu.VMEM((5, cz // 8 + 6, 8, rows), f32),
            pltpu.VMEM((5, ny + 6, 8, cz), f32),
            pltpu.VMEM((5, ny + 6, 8, cz), f32),
            pltpu.VMEM((ny // 8, 5, cx + 6, 8, cz), f32),
            pltpu.VMEM((ny // 8, 5, cx + 6, 8, cz), f32),
            pltpu.SemaphoreType.DMA,
            pltpu.SemaphoreType.DMA((2,)),
            pltpu.SemaphoreType.DMA,
            pltpu.SemaphoreType.DMA,
            pltpu.SemaphoreType.DMA((4,)),
            pltpu.SemaphoreType.DMA((4,)),
            pltpu.SemaphoreType.DMA,
        ],
        compiler_params=pltpu.CompilerParams(collective_id=0, has_side_effects=True),
        name="step",
    )(flat, top_ghost.transpose(0, 2, 1, 3), flags.transpose(0, 2, 1))
    new_register = REGISTER_DECAY * register - change.reshape(state.shape)
    new_state = state + UPDATE_WEIGHT * new_register
    return new_state, new_register


def solution(mesh):
    block = P(None, "gx", None, "gz")
    return jax.shard_map(
        functools.partial(shards, mesh.shape["gx"], mesh.shape["gz"]),
        mesh=mesh,
        in_specs=(block, block, block, P("gx", None, "gz")),
        out_specs=(block, block),
        check_vma=False,
    )
```

profile of v0, /device:TPU:0, one launch (start us, length us, event | category | flops | bytes accessed | tf_op | source)
XLA Modules:
  0.0 16.0 jit_solution(11628981123872618397)
XLA Ops:
  0.6 0.0 copy-start
  0.6 0.0 copy-start.1
  0.7 14.3 %step.1 = f32[5,128,128]{2,1,0:T(8,128)S(1)} custom-call(f32[5,128,128]{2,1,0:T(8,128)} %bitcast.7, f32[5,3,8,128]{3,2,1,0:T(8,128)} %bitcast.8, s32[8,1,16]{2,1,0:T(1,128)} %bitcast.9), custom_call_target="tpu_custom_call" | custom-call | tf_op jit(solution)/shard_map/step/pallas_call | solution.py:266
  15.0 0.0 copy-done
  15.0 0.0 copy-done.1
  15.0 0.9 %multiply_add_fusion = (f32[5,8,16,128]{3,2,1,0:T(8,128)}, f32[5,8,16,128]{3,2,1,0:T(8,128)}) fusion(f32[5,8,16,128]{3,2,1,0:T(8,128)S(1)} %copy-done, f32[5,8,16,128]{3,2,1,0:T(8,128)S(1)} %bitcast.6, f32[5,8,16,128]{3,2,1,0:T(8,128)S(1)} %copy-done.1), kind=kLoop, calls=%fused_computation | loop fusion | flops 327680 | bytes 1638400 | tf_op jit(solution)/shard_map/add | solution.py:298
Async XLA Ops:
  0.6 14.4 %copy-start = (f32[5,8,16,128]{3,2,1,0:T(8,128)S(1)}, f32[5,8,16,128]{3,2,1,0:T(8,128)}, u32[]{:S(2)}) copy-start(f32[5,8,16,128]{3,2,1,0:T(8,128)} %param.4) | copy-start | bytes 983044
  0.6 14.4 %copy-start.1 = (f32[5,8,16,128]{3,2,1,0:T(8,128)S(1)}, f32[5,8,16,128]{3,2,1,0:T(8,128)}, u32[]{:S(2)}) copy-start(f32[5,8,16,128]{3,2,1,0:T(8,128)} %param.5) | copy-start | bytes 983044
where the time goes:
time: 16.1 us; the launch traced here: 16 us
  Pallas kernels  14.3 us (89%)
  other arithmetic  0.92 us (6%)
  between operations  0.67 us (4%)
    pallas_call x1, Pallas kernels, shards(): pl.pallas_call(functools.partial(step_kernel, ngx, ngz, cx, ny), out_shap...  14.3 us
    add x1, other arithmetic, shards(): new_state = state + UPDATE_WEIGHT * new_register  0.92 us

commit v1 on v0

v1 whole, which is shorter than its diff:
```python
import functools

import jax
import jax.numpy as jnp
from jax import lax
from jax.experimental import pallas as pl
from jax.experimental.pallas import tpu as pltpu
from jax.sharding import PartitionSpec as P

MESH = pl.DeviceIdType.MESH
GAMMA = 1.4
EPS_WENO = 1e-06
LAMBDA = (0.1, 0.15, 0.1)
REGISTER_DECAY = -5.0 / 9.0
UPDATE_WEIGHT = 15.0 / 16.0
UNROLL_LIMIT = 64


def reciprocal(value):
    return pltpu.reciprocal(value, approx=False)


def pressure_velocity(cons):
    inverse = reciprocal(cons[0])
    vel = [cons[1] * inverse, cons[2] * inverse, cons[3] * inverse]
    pressure = (GAMMA - 1.0) * (
        cons[4] - 0.5 * (cons[1] * vel[0] + cons[2] * vel[1] + cons[3] * vel[2])
    )
    return inverse, vel, pressure


def shifted(me, step, count):
    moved = me + step
    return jnp.where(moved >= count, moved - count, moved)


def exchange_peers(gx, gz, ngx, ngz):
    offsets = [(dx, dz) for dx in range(ngx) for dz in range(ngz)][1:]

    def each_peer(action):
        if len(offsets) < UNROLL_LIMIT:
            for slot, (dx, dz) in enumerate(offsets):
                action(slot, shifted(gx, dx, ngx), shifted(gz, dz, ngz))
        else:
            def body(slot, carry):
                dx, dz = (slot + 1) // ngz, (slot + 1) % ngz
                action(slot, shifted(gx, dx, ngx), shifted(gz, dz, ngz))
                return carry
            lax.fori_loop(0, len(offsets), body, 0)

    return each_peer, len(offsets)


class Line:
    def __init__(self, load):
        cached = functools.lru_cache(None)
        self.load = cached(load)
        self.D = cached(lambda j: self.load(j + 1) - self.load(j))
        self.S = cached(lambda j: self.D(j) - self.D(j - 1))
        self.T = cached(lambda j: self.S(j + 1) - self.S(j))
        self.S2 = cached(lambda j: self.S(j) + self.S(j))
        self.C = cached(
            lambda j: (self.S(j) * self.S(j) * (4.0 / 3.0) + 4.0 * EPS_WENO)
            + self.D(j) * self.D(j - 1)
        )

    def L(self, j):
        return self.C(j) + self.S2(j) * self.D(j)

    def R(self, j):
        return self.C(j) - self.S2(j) * self.D(j - 1)


def correction(near, mid, far, t_near, t_far):
    a, b, c = mid * far, near * far, near * mid
    w_near = a * a
    w_far = 3.0 * (c * c)
    total = w_near + 6.0 * (b * b) + w_far
    return (w_far * t_far + (w_near + w_near) * t_near) * reciprocal(total)


def upwind_gaps(alpha, load_flux, load_cons):
    flux = functools.lru_cache(None)(load_flux)
    drift = functools.lru_cache(None)(lambda j: alpha * load_cons(j))
    plus, minus = Line(lambda j: flux(j) + drift(j)), Line(lambda j: flux(j) - drift(j))

    def gap(j):
        up = correction(plus.L(j - 1), plus.C(j), plus.R(j + 1), plus.T(j - 1), plus.T(j))
        down = correction(minus.R(j + 2), minus.C(j + 1), minus.L(j), minus.T(j + 1), minus.T(j))
        return 0.5 * (plus.T(j) - minus.T(j)) - up + down

    return gap


def difference_weights(flagged):
    return (
        jnp.where(flagged, 8.0, 9.0),
        jnp.where(flagged, -1.0, -1.8),
        jnp.where(flagged, 0.0, 0.2),
    )


def linear_part(weights, flux, cell):
    total = None
    for reach, weight in enumerate(weights, 1):
        high, low = flux(cell + reach), flux(cell - reach)
        if high is None and low is None:
            continue
        gap = -low if high is None else high if low is None else high - low
        total = weight * gap if total is None else total + weight * gap
    return total


def fluxes_of(cons, var):
    _, vel, pressure = pressure_velocity(cons)
    velocity = vel[var - 1]
    fluxes = [cons[field] * velocity for field in range(4)]
    fluxes.append((cons[4] + pressure) * velocity)
    fluxes[var] = fluxes[var] + pressure
    return fluxes


def store_fluxes(cons, var, fluxes, conserved, cell):
    for field, flux in enumerate(fluxes_of(cons, var)):
        fluxes[field, cell] = flux
        conserved[field, cell] = cons[field]


def halo_fluxes(cx, ny, part, xpad, xf):
    for cell in (0, 1, 2, cx + 3, cx + 4, cx + 5):
        cons = [xpad[f, pl.ds(cell * ny + part * 8, 8), :] for f in range(5)]
        for field, flux in enumerate(fluxes_of(cons, 1)):
            xf[field, cell] = flux


def edge_update(cx, ny, part, f, alpha, xpad, xf, mask, acc, emit):
    rows = lambda cell: pl.ds(cell * ny + part * 8, 8)
    gap = upwind_gaps(alpha, lambda j: xf[f, j + 3], lambda j: xpad[f, rows(j + 3), :])
    outside = lambda j: xf[f, j + 3] if j < 0 or j >= cx else None
    for cell in range(cx):
        total = acc[f, rows(cell), :]
        if cell < 3 or cell >= cx - 3:
            scaled = mask[rows(cell), :]
            weights = difference_weights(scaled > 0.0)
            missing = linear_part([w * (LAMBDA[0] / 12.0) for w in weights], outside, cell)
            jump = None
            if cell < 2 or cell >= cx - 3:
                jump = gap(cell)
            if cell < 3 or cell > cx - 3:
                jump = -gap(cell - 1) if jump is None else jump - gap(cell - 1)
            total = total - (missing + scaled * jump)
        emit(cell, total)


def exchange_kernel(
    ngx, ngz, cx, ny, state_ref, register_ref, ghost_ref, flags_ref,
    acc, xpad, xf, mask, top_ref, early_register, early_state,
    zt, reg, ghost, flags, slots, mine, acc_t, zf, zu, yf, yu, xf_early,
    load_sem, side_sem, send_sem, recv_sem, halo_send, halo_recv
):
    gx, gz = lax.axis_index("gx"), lax.axis_index("gz")
    parts = ny // 8
    rows = cx * ny
    halo = 3 * ny
    strip = zt.shape[1] - 16
    chunk = strip // 8
    load = pltpu.make_async_copy(state_ref, xpad.at[:, pl.ds(halo, rows), :], load_sem)
    load.start()
    load_flags = pltpu.make_async_copy(flags_ref, flags, side_sem.at[0])
    load_flags.start()
    load_ghost = pltpu.make_async_copy(ghost_ref, ghost, side_sem.at[1])
    load_ghost.start()
    load_register = pltpu.make_async_copy(register_ref, reg, side_sem.at[2])
    load_register.start()
    barrier = pltpu.get_barrier_semaphore()
    each_peer, peers = exchange_peers(gx, gz, ngx, ngz)

    def greet(slot, tx, tz):
        pl.semaphore_signal(barrier, inc=1, device_id=(tx, tz), device_id_type=MESH)

    each_peer(greet)
    load.wait()
    best = None
    for row in range(0, rows, 8):
        cons = [xpad[var, pl.ds(halo + row, 8), :] for var in range(5)]
        inverse, vel, pressure = pressure_velocity(cons)
        sound = jnp.sqrt(GAMMA * pressure * inverse)
        local = [jnp.abs(v) + sound for v in vel]
        best = local if best is None else [jnp.maximum(a, b) for a, b in zip(best, local)]
    tops = [jnp.max(jnp.max(b, axis=0, keepdims=True), axis=1, keepdims=True) for b in best]
    lane = lax.broadcasted_iota(jnp.int32, (1, 128), 1)
    mine[...] = jnp.where(lane == 0, tops[0], jnp.where(lane == 1, tops[1], tops[2]))

    pl.semaphore_wait(barrier, peers)

    def send(slot, tx, tz):
        pltpu.make_async_remote_copy(
            src_ref=mine, dst_ref=slots.at[slot], send_sem=send_sem, recv_sem=recv_sem,
            device_id=(tx, tz), device_id_type=MESH,
        ).start()

    each_peer(send)
    right, left = shifted(gx, 1, ngx), shifted(gx, ngx - 1, ngx)
    high, low = shifted(gz, 1, ngz), shifted(gz, ngz - 1, ngz)

    def move(index, src, dst, target):
        copy = pltpu.make_async_remote_copy(
            src_ref=src, dst_ref=dst, send_sem=halo_send.at[index], recv_sem=halo_recv.at[index],
            device_id=target, device_id_type=MESH,
        )
        copy.start()
        return copy

    blocks = xpad.reshape(5, cx + 6, ny, xpad.shape[2])
    x_copies = []
    for part in range(parts):
        layers = lambda first: blocks.at[:, pl.ds(first, 3), pl.ds(part * 8, 8), :]
        x_copies.append((
            move(2 + 2 * part, layers(3), layers(3 + cx), (left, gz)),
            move(3 + 2 * part, layers(cx), layers(0), (right, gz)),
        ))
    for var in range(5):
        zt[var, pl.ds(8, strip), :] = xpad[var, pl.ds(halo, rows), :].T
    z_copies = [
        move(0, zt.at[:, pl.ds(8, 8), :], zt.at[:, pl.ds(8 + strip, 8), :], (gx, low)),
        move(1, zt.at[:, pl.ds(strip, 8), :], zt.at[:, pl.ds(0, 8), :], (gx, high)),
    ]
    load_flags.wait()
    for x in range(cx):
        wide = jnp.broadcast_to(flags[x], (strip, ny)).astype(jnp.float32).T * (LAMBDA[0] / 12.0)
        mask[pl.ds(x * ny, ny), :] = wide
    mask_t = mask[...].T[:8]
    flag_t = mask_t > 0.0

    load_ghost.wait()
    for cell in range(ny + 6):
        y = cell - 3
        if y < ny:
            source = y if y >= 0 else -1 - y
            cons = [xpad[f, pl.ds(halo + source, 8, stride=ny), :] for f in range(5)]
            if y < 0:
                cons[2] = -cons[2]
        else:
            cons = [ghost[f, y - ny] for f in range(5)]
        store_fluxes(cons, 2, yf, yu, cell)
    load_register.wait()

    def y_linear(f, carry):
        for cell in range(ny):
            where = pl.ds(cell, 8, stride=ny)
            weights = difference_weights(mask[where, :] > 0.0)
            linear = linear_part(weights, lambda j: yf[f, j + 3], cell)
            acc[f, where, :] = REGISTER_DECAY * reg[f, where, :] - (LAMBDA[1] / 12.0) * linear
        return carry

    lax.fori_loop(0, 5, y_linear, 0)
    for part in range(parts):
        target = xf if part == parts - 1 else xf_early.at[part]
        for cell in range(cx):
            cons = [xpad[f, pl.ds(halo + cell * ny + part * 8, 8), :] for f in range(5)]
            for field, flux in enumerate(fluxes_of(cons, 1)):
                target[field, 3 + cell] = flux

    def x_linear(f, carry):
        for part in range(parts):
            source = xf if part == parts - 1 else xf_early.at[part]
            inside = lambda j: source[f, j + 3] if 0 <= j < cx else None
            for cell in range(cx):
                where = pl.ds(cell * ny + part * 8, 8)
                weights = difference_weights(mask[where, :] > 0.0)
                linear = linear_part(weights, inside, cell)
                acc[f, where, :] = acc[f, where, :] - (LAMBDA[0] / 12.0) * linear
        return carry

    lax.fori_loop(0, 5, x_linear, 0)

    for copy in z_copies:
        copy.wait()
    for cell in range(chunk + 6):
        cons = [zt[f, pl.ds(5 + cell, 8, stride=chunk), :] for f in range(5)]
        store_fluxes(cons, 3, zf, zu, cell)
    weights_t = [w * (-LAMBDA[2] / 12.0) for w in difference_weights(flag_t)]

    def z_linear(f, carry):
        for cell in range(chunk):
            linear = linear_part(weights_t, lambda j: zf[f, j + 3], cell)
            acc_t[f, pl.ds(cell, 8, stride=chunk), :] = linear
        return carry

    lax.fori_loop(0, 5, z_linear, 0)

    pltpu.make_async_copy(slots, slots, recv_sem).wait()
    top = jnp.maximum(jnp.max(slots[...], axis=0), mine[...])
    top_ref[...] = jnp.broadcast_to(top, (8, 128))
    alpha = [jnp.broadcast_to(top[:, k : k + 1], (8, 128)) for k in range(3)]

    def z_field(f, carry):
        gap = upwind_gaps(alpha[2], lambda j: zf[f, j + 3], lambda j: zu[f, j + 3])
        before = gap(-1)
        for cell in range(chunk):
            after = gap(cell)
            where = pl.ds(cell, 8, stride=chunk)
            acc_t[f, where, :] = acc_t[f, where, :] - mask_t * (after - before)
            before = after
        return carry

    lax.fori_loop(0, 5, z_field, 0)

    def y_field(f, carry):
        gap = upwind_gaps(alpha[1], lambda j: yf[f, j + 3], lambda j: yu[f, j + 3])
        acc[f] = acc[f] + acc_t[f].T
        before = gap(-1)
        for cell in range(ny):
            after = gap(cell)
            where = pl.ds(cell, 8, stride=ny)
            scaled = (LAMBDA[1] / LAMBDA[0]) * mask[where, :]
            acc[f, where, :] = acc[f, where, :] - scaled * (after - before)
            before = after
        return carry

    lax.fori_loop(0, 5, y_field, 0)

    def x_field(f, carry):
        for part in range(parts):
            source = xf if part == parts - 1 else xf_early.at[part]
            at = lambda cell: pl.ds(cell * ny + part * 8, 8)
            gap = upwind_gaps(
                alpha[0], lambda j: source[f, j + 3], lambda j: xpad[f, at(j + 3), :]
            )
            for cell in range(2, cx - 2):
                if cell == 2:
                    jump = gap(2)
                elif cell == cx - 3:
                    jump = -gap(cell - 1)
                else:
                    jump = gap(cell) - gap(cell - 1)
                acc[f, at(cell), :] = acc[f, at(cell), :] - mask[at(cell), :] * jump
        return carry

    lax.fori_loop(0, 5, x_field, 0)

    for part in range(parts):
        for copy in x_copies[part]:
            copy.wait()
        if part < parts - 1:
            halo_fluxes(cx, ny, part, xpad, xf_early.at[part])

            def early(f, carry):
                def emit(cell, total):
                    state = xpad[f, pl.ds(halo + cell * ny + part * 8, 8), :]
                    early_register[part, f, cell] = total
                    early_state[part, f, cell] = state + UPDATE_WEIGHT * total
                edge_update(cx, ny, part, f, alpha[0], xpad, xf_early.at[part], mask, acc, emit)
                return carry

            lax.fori_loop(0, 5, early, 0)
    pltpu.make_async_copy(slots, slots, send_sem).wait()


def update_kernel(
    cx, ny, acc, xpad, xf_in, mask, top_ref, early_register, early_state,
    state_out, register_out, xf, late_register, late_state, sems
):
    parts = ny // 8
    part = parts - 1
    copies = []

    def put(src, dst):
        copy = pltpu.make_async_copy(src, dst, sems.at[len(copies)])
        copy.start()
        copies.append(copy)

    for p in range(parts - 1):
        put(early_register.at[p], register_out.at[:, :, pl.ds(p * 8, 8), :])
        put(early_state.at[p], state_out.at[:, :, pl.ds(p * 8, 8), :])
    halo_fluxes(cx, ny, part, xpad, xf)
    for f in range(5):
        for cell in range(3, cx + 3):
            xf[f, cell] = xf_in[f, cell]
    alpha = jnp.broadcast_to(top_ref[:, 0:1], (8, 128))
    for f in range(5):
        def emit(cell, total):
            state = xpad[f, pl.ds((3 + cell) * ny + part * 8, 8), :]
            late_register[f, cell] = total
            late_state[f, cell] = state + UPDATE_WEIGHT * total
        edge_update(cx, ny, part, f, alpha, xpad, xf, mask, acc, emit)
        put(late_register.at[f], register_out.at[f, :, pl.ds(part * 8, 8), :])
        put(late_state.at[f], state_out.at[f, :, pl.ds(part * 8, 8), :])
    for copy in copies:
        copy.wait()


def shards(ngx, ngz, state, register, top_ghost, flags):
    _, cx, ny, cz = state.shape
    rows = cx * ny
    parts = ny // 8
    peers = ngx * ngz - 1
    f32 = jnp.float32
    flat = lambda array: array.reshape(5, rows, cz)
    anywhere = pl.BlockSpec(memory_space=pl.ANY)
    inside = pl.BlockSpec(memory_space=pltpu.VMEM)
    held = pl.pallas_call(
        functools.partial(exchange_kernel, ngx, ngz, cx, ny),
        out_shape=(
            pltpu.VMEM((5, rows, cz), f32),
            pltpu.VMEM((5, (cx + 6) * ny, cz), f32),
            pltpu.VMEM((5, cx + 6, 8, cz), f32),
            pltpu.VMEM((rows, cz), f32),
            pltpu.VMEM((8, 128), f32),
            pltpu.VMEM((max(parts - 1, 1), 5, cx, 8, cz), f32),
            pltpu.VMEM((max(parts - 1, 1), 5, cx, 8, cz), f32),
        ),
        in_specs=[anywhere] * 4,
        out_specs=(inside,) * 7,
        scratch_shapes=[
            pltpu.VMEM((5, cz + 16, rows), f32),
            pltpu.VMEM((5, rows, cz), f32),
            pltpu.VMEM((5, 3, cx, cz), f32),
            pltpu.VMEM((cx, 1, ny), jnp.int32),
            pltpu.VMEM((peers, 1, 128), f32),
            pltpu.VMEM((1, 128), f32),
            pltpu.VMEM((5, cz, rows), f32),
            pltpu.VMEM((5, cz // 8 + 6, 8, rows), f32),
            pltpu.VMEM((5, cz // 8 + 6, 8, rows), f32),
            pltpu.VMEM((5, ny + 6, cx, cz), f32),
            pltpu.VMEM((5, ny + 6, cx, cz), f32),
            pltpu.VMEM((max(parts - 1, 1), 5, cx + 6, 8, cz), f32),
            pltpu.SemaphoreType.DMA,
            pltpu.SemaphoreType.DMA((3,)),
            pltpu.SemaphoreType.DMA,
            pltpu.SemaphoreType.DMA,
            pltpu.SemaphoreType.DMA((2 + 2 * parts,)),
            pltpu.SemaphoreType.DMA((2 + 2 * parts,)),
        ],
        compiler_params=pltpu.CompilerParams(collective_id=0, has_side_effects=True),
        name="exchange",
    )(flat(state), flat(register), top_ghost.transpose(0, 2, 1, 3), flags.transpose(0, 2, 1))
    block = jax.ShapeDtypeStruct(state.shape, f32)
    return pl.pallas_call(
        functools.partial(update_kernel, cx, ny),
        out_shape=(block, block),
        in_specs=[inside] * 7,
        out_specs=(anywhere, anywhere),
        scratch_shapes=[
            pltpu.VMEM((5, cx + 6, 8, cz), f32),
            pltpu.VMEM((5, cx, 8, cz), f32),
            pltpu.VMEM((5, cx, 8, cz), f32),
            pltpu.SemaphoreType.DMA((2 * (parts - 1) + 10,)),
        ],
        name="update",
    )(*(pltpu.with_memory_space_constraint(array, pltpu.VMEM) for array in held))


def solution(mesh):
    block = P(None, "gx", None, "gz")
    return jax.shard_map(
        functools.partial(shards, mesh.shape["gx"], mesh.shape["gz"]),
        mesh=mesh,
        in_specs=(block, block, block, P("gx", None, "gz")),
        out_specs=(block, block),
        check_vma=False,
    )
```

time: 16.1 us -> 15.3 us (0.950)
  other arithmetic: 0.92 us -> 0 us
  Pallas kernels: 14.3 us -> 14.5 us
    add x1 -> x0, other arithmetic: 0.92 us -> none  [shards(): new_state = state + UPDATE_WEIGHT * new_register]
    pallas_call x1 -> x2, Pallas kernels: 14.3 us -> 14.5 us  [the longest x1 13.3 us: shards(): pl.pallas_call(functools.partial(exchange_kernel, ngx, ngz, cx, ny), out_...]
where the time goes in v1:
time: 15.3 us; the launch traced here: 15.2 us
  Pallas kernels  14.5 us (95%)
  between operations  0.64 us (4%)
    pallas_call x1, Pallas kernels, shards(): pl.pallas_call(functools.partial(exchange_kernel, ngx, ngz, cx, ny), out_...  13.3 us
    pallas_call x1, Pallas kernels, shards(): pl.pallas_call(functools.partial(update_kernel, cx, ny), out_shape=(block...  1.19 us

profile of v1, /device:TPU:0, one launch (start us, length us, event | category | flops | bytes accessed | tf_op | source)
XLA Modules:
  0.0 15.2 jit_solution(4885297207251848357)
XLA Ops:
  0.6 13.3 %exchange.1 = (f32[5,128,128]{2,1,0:T(8,128)S(1)}, f32[5,224,128]{2,1,0:T(8,128)S(1)}, f32[5,14,8,128]{3,2,1,0:T(8,128)S(1)}, f32[128,128]{1,0:T(8,128)S(1)}, f3...) custom-call(f32[5,128,128]{2,1,0:T(8,128)} %bitcast.6, ...), custom_call_target="tpu_custom_call" | custom-call | tf_op jit(solution)/shard_map/exchange/pallas_call | solution.py:402
  14.0 1.2 %update.1 = (f32[5,8,16,128]{3,2,1,0:T(8,128)}, f32[5,8,16,128]{3,2,1,0:T(8,128)}) custom-call(f32[5,128,128]{2,1,0:T(8,128)S(1)} %get-tuple-element.9.acc, f32[5,224,128]{2,1,0:T(8,128)S(1)} %get-tuple-element.10.xpad, f32[5,14,8,128]{3,2,1,0:T(8,128)S(1)} %get-tuple-element.11.xf_in, f32[128,128]{1,0:T(8,128)S(1)} %get-tuple-element.12.mask, ...), custom_call_target="tpu_custom_call" | custom-call | tf_op jit(solution)/shard_map/update/pallas_call | solution.py:439

commit v2 on v1

--- a/solution.py
+++ b/solution.py
@@ -14,6 +14,7 @@
 REGISTER_DECAY = -5.0 / 9.0
 UPDATE_WEIGHT = 15.0 / 16.0
 UNROLL_LIMIT = 64
+MID = 6.0**-0.5
 
 
 def reciprocal(value):
@@ -34,26 +35,81 @@
     return jnp.where(moved >= count, moved - count, moved)
 
 
-def exchange_peers(gx, gz, ngx, ngz):
-    offsets = [(dx, dz) for dx in range(ngx) for dz in range(ngz)][1:]
-
-    def each_peer(action):
-        if len(offsets) < UNROLL_LIMIT:
-            for slot, (dx, dz) in enumerate(offsets):
-                action(slot, shifted(gx, dx, ngx), shifted(gz, dz, ngz))
-        else:
-            def body(slot, carry):
-                dx, dz = (slot + 1) // ngz, (slot + 1) % ngz
-                action(slot, shifted(gx, dx, ngx), shifted(gz, dz, ngz))
-                return carry
-            lax.fori_loop(0, len(offsets), body, 0)
-
-    return each_peer, len(offsets)
+def each(count, action, unroll):
+    if unroll:
+        for index in range(count):
+            action(index)
+    else:
+        def body(index, carry):
+            action(index)
+            return carry
+        lax.fori_loop(0, count, body, 0)
+
+
+def plane_size(ngx):
+    return max(p for p in range(1, ngx + 1) if ngx % p == 0 and p * p <= ngx)
+
+
+class Peers:
+    def __init__(self, ngx, ngz):
+        self.ngx, self.ngz = ngx, ngz
+        self.gx, self.gz = lax.axis_index("gx"), lax.axis_index("gz")
+        self.wide = plane_size(ngx)
+        self.planes = ngx // self.wide
+        self.members = self.wide * ngz
+        self.q, self.r = lax.div(self.gx, self.wide), lax.rem(self.gx, self.wide)
+        self.own = self.r * ngz + self.gz
+        self.last = self.gx == ngx - 1
+        self.unroll = self.planes * self.members < UNROLL_LIMIT
+
+    def member(self, plane, index):
+        if isinstance(index, int):
+            return plane * self.wide + index // self.ngz, index % self.ngz
+        return plane * self.wide + lax.div(index, self.ngz), lax.rem(index, self.ngz)
+
+    def plane_mates(self, action):
+        def visit(index):
+            @pl.when(self.own != index)
+            def _():
+                action(index, *self.member(self.q, index))
+        each(self.members, visit, self.unroll)
+
+    def of_planes(self, wanted, action):
+        def visit(plane):
+            @pl.when(wanted(plane))
+            def _():
+                each(self.members, lambda index: action(index, *self.member(plane, index)), self.unroll)
+        each(self.planes, visit, self.unroll)
+
+    def columns(self, wanted, action):
+        def visit(plane):
+            @pl.when(wanted(plane))
+            def _():
+                action(plane, (plane * self.wide + self.r, self.gz))
+        each(self.planes, visit, self.unroll)
+
+    def greet(self, barrier):
+        def signal(tx, tz):
+            pl.semaphore_signal(barrier, inc=1, device_id=(tx, tz), device_id_type=MESH)
+
+        @pl.when((self.r == 0) & (self.gx > 0))
+        def _():
+            signal(self.gx - 1, self.gz)
+
+        self.plane_mates(lambda index, tx, tz: signal(tx, tz))
+        self.of_planes(lambda plane: plane > self.q, lambda index, tx, tz: signal(tx, tz))
+
+    def greetings(self):
+        has_next = (self.r == self.wide - 1) & jnp.logical_not(self.last)
+        return self.members - 1 + self.q * self.members + has_next.astype(jnp.int32)
+
+
+def cached(function):
+    return functools.lru_cache(None)(function)
 
 
 class Line:
     def __init__(self, load):
-        cached = functools.lru_cache(None)
         self.load = cached(load)
         self.D = cached(lambda j: self.load(j + 1) - self.load(j))
         self.S = cached(lambda j: self.D(j) - self.D(j - 1))
@@ -63,33 +119,106 @@
             lambda j: (self.S(j) * self.S(j) * (4.0 / 3.0) + 4.0 * EPS_WENO)
             + self.D(j) * self.D(j - 1)
         )
-
-    def L(self, j):
-        return self.C(j) + self.S2(j) * self.D(j)
-
-    def R(self, j):
-        return self.C(j) - self.S2(j) * self.D(j - 1)
+        self.L = cached(lambda j: self.C(j) + self.S2(j) * self.D(j))
+        self.M = cached(lambda j: MID * self.C(j))
+        self.R = cached(lambda j: self.C(j) - self.S2(j) * self.D(j - 1))
 
 
 def correction(near, mid, far, t_near, t_far):
     a, b, c = mid * far, near * far, near * mid
     w_near = a * a
     w_far = 3.0 * (c * c)
-    total = w_near + 6.0 * (b * b) + w_far
+    total = w_near + b * b + w_far
     return (w_far * t_far + (w_near + w_near) * t_near) * reciprocal(total)
 
 
-def upwind_gaps(alpha, load_flux, load_cons):
-    flux = functools.lru_cache(None)(load_flux)
-    drift = functools.lru_cache(None)(lambda j: alpha * load_cons(j))
-    plus, minus = Line(lambda j: flux(j) + drift(j)), Line(lambda j: flux(j) - drift(j))
-
+def face_gap(plus, minus, drift_t):
     def gap(j):
-        up = correction(plus.L(j - 1), plus.C(j), plus.R(j + 1), plus.T(j - 1), plus.T(j))
-        down = correction(minus.R(j + 2), minus.C(j + 1), minus.L(j), minus.T(j + 1), minus.T(j))
-        return 0.5 * (plus.T(j) - minus.T(j)) - up + down
+        up = correction(plus.L(j - 1), plus.M(j), plus.R(j + 1), plus.T(j - 1), plus.T(j))
+        down = correction(minus.R(j + 2), minus.M(j + 1), minus.L(j), minus.T(j + 1), minus.T(j))
+        return drift_t(j) - up + down
 
     return gap
+
+
+KINDS = ("L", "M", "R")
+
+
+def prepare(flux, cons, cells, store):
+    f, u = Line(flux), Line(cons)
+    for j in cells:
+        mixed = (8.0 / 3.0) * (f.S(j) * u.S(j)) + (f.D(j) * u.D(j - 1) + f.D(j - 1) * u.D(j))
+        curved = (4.0 / 3.0) * (u.S(j) * u.S(j)) + u.D(j) * u.D(j - 1)
+        centre = (f.C(j), mixed, curved)
+
+        def product(at):
+            return (
+                f.S2(j) * f.D(at),
+                f.S2(j) * u.D(at) + u.S2(j) * f.D(at),
+                u.S2(j) * u.D(at),
+            )
+
+        left = [c + p for c, p in zip(centre, product(j))]
+        right = [c - p for c, p in zip(centre, product(j - 1))]
+        for kind, terms in enumerate((left, [MID * c for c in centre], right)):
+            for power, term in enumerate(terms):
+                store(3 * kind + power, j, term)
+
+
+def prepare_third(flux, cons, cells, store):
+    f, u = Line(flux), Line(cons)
+    for j in cells:
+        store(9, j, f.T(j))
+        store(10, j, u.T(j))
+
+
+class Prepared:
+    def __init__(self, alpha, load):
+        square = alpha * alpha
+
+        def both(kind):
+            def pair(j):
+                even = load(3 * kind, j) + square * load(3 * kind + 2, j)
+                odd = alpha * load(3 * kind + 1, j)
+                return even + odd, even - odd
+            return cached(pair)
+
+        self.drift_t = cached(lambda j: alpha * load(10, j))
+        third = cached(lambda j: (load(9, j) + self.drift_t(j), load(9, j) - self.drift_t(j)))
+        pairs = {name: both(kind) for kind, name in enumerate(KINDS)} | {"T": third}
+        self.side = [
+            {name: (lambda j, pair=pair, k=k: pair(j)[k]) for name, pair in pairs.items()} for k in range(2)
+        ]
+
+
+class Side:
+    def __init__(self, values):
+        self.L, self.M, self.R, self.T = (values[name] for name in (*KINDS, "T"))
+
+
+def prepared_gaps(alpha, load):
+    ready = Prepared(alpha, load)
+    return face_gap(Side(ready.side[0]), Side(ready.side[1]), ready.drift_t)
+
+
+def edge_gaps(alpha, load_flux, load_cons, load, inner, inner_t):
+    flux = cached(load_flux)
+    drift = cached(lambda j: alpha * load_cons(j))
+    ready = Prepared(alpha, load)
+    fresh = Line(lambda j: flux(j) + drift(j)), Line(lambda j: flux(j) - drift(j))
+
+    def mixed(k):
+        def pick(name):
+            known = inner_t if name == "T" else inner
+            return lambda j: ready.side[k][name](j) if j in known else getattr(fresh[k], name)(j)
+        return Side({name: pick(name) for name in (*KINDS, "T")})
+
+    plus, minus = mixed(0), mixed(1)
+
+    def drift_t(j):
+        return ready.drift_t(j) if j in inner_t else 0.5 * (plus.T(j) - minus.T(j))
+
+    return face_gap(plus, minus, drift_t)
 
 
 def difference_weights(flagged):
@@ -126,6 +255,15 @@
         conserved[field, cell] = cons[field]
 
 
+def prepare_line(count, f, fluxes, conserved, out):
+    def keep(kind, j, value):
+        out[kind, f, j + 2] = value
+
+    flux, cons = cached(lambda j: fluxes[f, j + 3]), cached(lambda j: conserved[f, j + 3])
+    prepare(flux, cons, range(-2, count + 2), keep)
+    prepare_third(flux, cons, range(-2, count + 1), keep)
+
+
 def halo_fluxes(cx, ny, part, xpad, xf):
     for cell in (0, 1, 2, cx + 3, cx + 4, cx + 5):
         cons = [xpad[f, pl.ds(cell * ny + part * 8, 8), :] for f in range(5)]
@@ -133,9 +271,12 @@
             xf[field, cell] = flux
 
 
-def edge_update(cx, ny, part, f, alpha, xpad, xf, mask, acc, emit):
+def edge_update(cx, ny, part, f, alpha, xpad, xf, mask, acc, near, emit):
     rows = lambda cell: pl.ds(cell * ny + part * 8, 8)
-    gap = upwind_gaps(alpha, lambda j: xf[f, j + 3], lambda j: xpad[f, rows(j + 3), :])
+    gap = edge_gaps(
+        alpha, lambda j: xf[f, j + 3], lambda j: xpad[f, rows(j + 3), :],
+        lambda k, j: near[k, f, j - 1], range(1, cx - 1), range(1, cx - 2),
+    )
     outside = lambda j: xf[f, j + 3] if j < 0 or j >= cx else None
     for cell in range(cx):
         total = acc[f, rows(cell), :]
@@ -154,11 +295,12 @@
 
 def exchange_kernel(
     ngx, ngz, cx, ny, state_ref, register_ref, ghost_ref, flags_ref,
-    acc, xpad, xf, mask, top_ref, early_register, early_state,
-    zt, reg, ghost, flags, slots, mine, acc_t, zf, zu, yf, yu, xf_early,
-    load_sem, side_sem, send_sem, recv_sem, halo_send, halo_recv
+    acc, xpad, xf, mask, top_ref, near, early_register, early_state,
+    zt, reg, ghost, flags, slots, mine, plane_top, acc_t, zf, zu, yf, yu, xf_early, near_early, yq, zq,
+    load_sem, side_sem, send_sem, recv_sem, halo_send, halo_recv, ready_up, ready_wrap
 ):
-    gx, gz = lax.axis_index("gx"), lax.axis_index("gz")
+    peers = Peers(ngx, ngz)
+    gx, gz = peers.gx, peers.gz
     parts = ny // 8
     rows = cx * ny
     halo = 3 * ny
@@ -172,13 +314,9 @@
     load_ghost.start()
     load_register = pltpu.make_async_copy(register_ref, reg, side_sem.at[2])
     load_register.start()
+    slots[...] = jnp.zeros(slots.shape, slots.dtype)
     barrier = pltpu.get_barrier_semaphore()
-    each_peer, peers = exchange_peers(gx, gz, ngx, ngz)
-
-    def greet(slot, tx, tz):
-        pl.semaphore_signal(barrier, inc=1, device_id=(tx, tz), device_id_type=MESH)
-
-    each_peer(greet)
+    peers.greet(barrier)
     load.wait()
     best = None
     for row in range(0, rows, 8):
@@ -191,40 +329,70 @@
     lane = lax.broadcasted_iota(jnp.int32, (1, 128), 1)
     mine[...] = jnp.where(lane == 0, tops[0], jnp.where(lane == 1, tops[1], tops[2]))
 
-    pl.semaphore_wait(barrier, peers)
-
-    def send(slot, tx, tz):
-        pltpu.make_async_remote_copy(
-            src_ref=mine, dst_ref=slots.at[slot], send_sem=send_sem, recv_sem=recv_sem,
-            device_id=(tx, tz), device_id_type=MESH,
-        ).start()
-
-    each_peer(send)
     right, left = shifted(gx, 1, ngx), shifted(gx, ngx - 1, ngx)
     high, low = shifted(gz, 1, ngz), shifted(gz, ngz - 1, ngz)
 
     def move(index, src, dst, target):
-        copy = pltpu.make_async_remote_copy(
+        return pltpu.make_async_remote_copy(
             src_ref=src, dst_ref=dst, send_sem=halo_send.at[index], recv_sem=halo_recv.at[index],
             device_id=target, device_id_type=MESH,
         )
-        copy.start()
-        return copy
 
     blocks = xpad.reshape(5, cx + 6, ny, xpad.shape[2])
-    x_copies = []
+    to_left, to_right = [], []
     for part in range(parts):
         layers = lambda first: blocks.at[:, pl.ds(first, 3), pl.ds(part * 8, 8), :]
-        x_copies.append((
-            move(2 + 2 * part, layers(3), layers(3 + cx), (left, gz)),
-            move(3 + 2 * part, layers(cx), layers(0), (right, gz)),
-        ))
+        to_left.append(move(2 + 2 * part, layers(3), layers(3 + cx), (left, gz)))
+        to_right.append(move(3 + 2 * part, layers(cx), layers(0), (right, gz)))
+
+    def start(copies):
+        for copy in copies:
+            copy.start()
+
+    def signal(semaphore, target):
+        pl.semaphore_signal(semaphore, inc=1, device_id=target, device_id_type=MESH)
+
+    def tell(source, plane, index, target):
+        pltpu.make_async_remote_copy(
+            src_ref=source, dst_ref=slots.at[peers.q, index], send_sem=send_sem.at[plane],
+            recv_sem=recv_sem.at[peers.q], device_id=target, device_id_type=MESH,
+        ).start()
+
+    pl.semaphore_wait(barrier, peers.greetings())
+
+    def tell_lower(plane):
+        @pl.when(plane < peers.q)
+        def _():
+            each(
+                peers.members,
+                lambda index: tell(mine, plane, peers.own, peers.member(plane, index)),
+                peers.unroll,
+            )
+
+    each(peers.planes, tell_lower, peers.unroll)
+    peers.plane_mates(lambda index, tx, tz: tell(mine, peers.q, peers.own, (tx, tz)))
+
+    @pl.when(peers.last)
+    def _():
+        start(to_right)
+        signal(ready_wrap, (0, gz))
+
+    @pl.when(gx > 0)
+    def _():
+        start(to_left)
+
+    @pl.when(jnp.logical_not(peers.last))
+    def _():
+        start(to_right)
+
+    peers.columns(lambda plane: plane < peers.q, lambda plane, target: signal(ready_up.at[peers.q], target))
     for var in range(5):
         zt[var, pl.ds(8, strip), :] = xpad[var, pl.ds(halo, rows), :].T
     z_copies = [
         move(0, zt.at[:, pl.ds(8, 8), :], zt.at[:, pl.ds(8 + strip, 8), :], (gx, low)),
         move(1, zt.at[:, pl.ds(strip, 8), :], zt.at[:, pl.ds(0, 8), :], (gx, high)),
     ]
+    start(z_copies)
     load_flags.wait()
     for x in range(cx):
         wide = jnp.broadcast_to(flags[x], (strip, ny)).astype(jnp.float32).T * (LAMBDA[0] / 12.0)
@@ -251,6 +419,7 @@
             weights = difference_weights(mask[where, :] > 0.0)
             linear = linear_part(weights, lambda j: yf[f, j + 3], cell)
             acc[f, where, :] = REGISTER_DECAY * reg[f, where, :] - (LAMBDA[1] / 12.0) * linear
+        prepare_line(ny, f, yf, yu, yq)
         return carry
 
     lax.fori_loop(0, 5, y_linear, 0)
@@ -264,7 +433,15 @@
     def x_linear(f, carry):
         for part in range(parts):
             source = xf if part == parts - 1 else xf_early.at[part]
+            found = near if part == parts - 1 else near_early.at[part]
             inside = lambda j: source[f, j + 3] if 0 <= j < cx else None
+
+            def keep(kind, j, value):
+                found[kind, f, j - 1] = value
+
+            at = lambda j: pl.ds((j + 3) * ny + part * 8, 8)
+            prepare(inside, lambda j: xpad[f, at(j), :], range(1, cx - 1), keep)
+            prepare_third(inside, lambda j: xpad[f, at(j), :], range(1, cx - 2), keep)
             for cell in range(cx):
                 where = pl.ds(cell * ny + part * 8, 8)
                 weights = difference_weights(mask[where, :] > 0.0)
@@ -285,17 +462,45 @@
         for cell in range(chunk):
             linear = linear_part(weights_t, lambda j: zf[f, j + 3], cell)
             acc_t[f, pl.ds(cell, 8, stride=chunk), :] = linear
+        prepare_line(chunk, f, zf, zu, zq)
         return carry
 
     lax.fori_loop(0, 5, z_linear, 0)
 
-    pltpu.make_async_copy(slots, slots, recv_sem).wait()
-    top = jnp.maximum(jnp.max(slots[...], axis=0), mine[...])
+    def all_of(plane, count, semaphores):
+        some = slots.at[plane, pl.ds(0, count)]
+        pltpu.make_async_copy(some, some, semaphores.at[plane]).wait()
+
+    all_of(peers.q, peers.members - 1, recv_sem)
+    plane_top[...] = jnp.maximum(jnp.max(slots[peers.q], axis=0), mine[...])
+
+    def tell_higher(plane, target):
+        pl.semaphore_wait(ready_up.at[plane], 1)
+        tell(plane_top, plane, 0, target)
+
+    peers.columns(lambda plane: plane > peers.q, tell_higher)
+
+    @pl.when(gx == 0)
+    def _():
+        pl.semaphore_wait(ready_wrap, 1)
+        start(to_left)
+
+    def arrivals(plane):
+        @pl.when(plane > peers.q)
+        def _():
+            all_of(plane, peers.members, recv_sem)
+
+        @pl.when(plane < peers.q)
+        def _():
+            all_of(plane, 1, recv_sem)
+
+    each(peers.planes, arrivals, peers.unroll)
+    top = jnp.maximum(jnp.max(jnp.max(slots[...], axis=0), axis=0), mine[...])
     top_ref[...] = jnp.broadcast_to(top, (8, 128))
     alpha = [jnp.broadcast_to(top[:, k : k + 1], (8, 128)) for k in range(3)]
 
     def z_field(f, carry):
-        gap = upwind_gaps(alpha[2], lambda j: zf[f, j + 3], lambda j: zu[f, j + 3])
+        gap = prepared_gaps(alpha[2], lambda k, j: zq[k, f, j + 2])
         before = gap(-1)
         for cell in range(chunk):
             after = gap(cell)
@@ -307,7 +512,7 @@
     lax.fori_loop(0, 5, z_field, 0)
 
     def y_field(f, carry):
-        gap = upwind_gaps(alpha[1], lambda j: yf[f, j + 3], lambda j: yu[f, j + 3])
+        gap = prepared_gaps(alpha[1], lambda k, j: yq[k, f, j + 2])
         acc[f] = acc[f] + acc_t[f].T
         before = gap(-1)
         for cell in range(ny):
@@ -322,11 +527,9 @@
 
     def x_field(f, carry):
         for part in range(parts):
-            source = xf if part == parts - 1 else xf_early.at[part]
+            found = near if part == parts - 1 else near_early.at[part]
             at = lambda cell: pl.ds(cell * ny + part * 8, 8)
-            gap = upwind_gaps(
-                alpha[0], lambda j: source[f, j + 3], lambda j: xpad[f, at(j + 3), :]
-            )
+            gap = prepared_gaps(alpha[0], lambda k, j: found[k, f, j - 1])
             for cell in range(2, cx - 2):
                 if cell == 2:
                     jump = gap(2)
@@ -340,8 +543,8 @@
     lax.fori_loop(0, 5, x_field, 0)
 
     for part in range(parts):
-        for copy in x_copies[part]:
-            copy.wait()
+        to_left[part].wait()
+        to_right[part].wait()
         if part < parts - 1:
             halo_fluxes(cx, ny, part, xpad, xf_early.at[part])
 
@@ -350,15 +553,28 @@
                     state = xpad[f, pl.ds(halo + cell * ny + part * 8, 8), :]
                     early_register[part, f, cell] = total
                     early_state[part, f, cell] = state + UPDATE_WEIGHT * total
-                edge_update(cx, ny, part, f, alpha[0], xpad, xf_early.at[part], mask, acc, emit)
+                edge_update(
+                    cx, ny, part, f, alpha[0], xpad, xf_early.at[part], mask, acc, near_early.at[part], emit
+                )
                 return carry
 
             lax.fori_loop(0, 5, early, 0)
-    pltpu.make_async_copy(slots, slots, send_sem).wait()
+
+    def departures(plane):
+        @pl.when(plane > peers.q)
+        def _():
+            all_of(plane, 1, send_sem)
+
+        @pl.when(plane < peers.q)
+        def _():
+            all_of(plane, peers.members, send_sem)
+
+    each(peers.planes, departures, peers.unroll)
+    all_of(peers.q, peers.members - 1, send_sem)
 
 
 def update_kernel(
-    cx, ny, acc, xpad, xf_in, mask, top_ref, early_register, early_state,
+    cx, ny, acc, xpad, xf_in, mask, top_ref, near, early_register, early_state,
     state_out, register_out, xf, late_register, late_state, sems
 ):
     parts = ny // 8
@@ -383,7 +599,7 @@
             state = xpad[f, pl.ds((3 + cell) * ny + part * 8, 8), :]
             late_register[f, cell] = total
             late_state[f, cell] = state + UPDATE_WEIGHT * total
-        edge_update(cx, ny, part, f, alpha, xpad, xf, mask, acc, emit)
+        edge_update(cx, ny, part, f, alpha, xpad, xf, mask, acc, near, emit)
         put(late_register.at[f], register_out.at[f, :, pl.ds(part * 8, 8), :])
         put(late_state.at[f], state_out.at[f, :, pl.ds(part * 8, 8), :])
     for copy in copies:
@@ -394,7 +610,7 @@
     _, cx, ny, cz = state.shape
     rows = cx * ny
     parts = ny // 8
-    peers = ngx * ngz - 1
+    wide = plane_size(ngx)
     f32 = jnp.float32
     flat = lambda array: array.reshape(5, rows, cz)
     anywhere = pl.BlockSpec(memory_space=pl.ANY)
@@ -407,17 +623,19 @@
             pltpu.VMEM((5, cx + 6, 8, cz), f32),
             pltpu.VMEM((rows, cz), f32),
             pltpu.VMEM((8, 128), f32),
+            pltpu.VMEM((11, 5, cx - 2, 8, cz), f32),
             pltpu.VMEM((max(parts - 1, 1), 5, cx, 8, cz), f32),
             pltpu.VMEM((max(parts - 1, 1), 5, cx, 8, cz), f32),
         ),
         in_specs=[anywhere] * 4,
-        out_specs=(inside,) * 7,
+        out_specs=(inside,) * 8,
         scratch_shapes=[
             pltpu.VMEM((5, cz + 16, rows), f32),
             pltpu.VMEM((5, rows, cz), f32),
             pltpu.VMEM((5, 3, cx, cz), f32),
             pltpu.VMEM((cx, 1, ny), jnp.int32),
-            pltpu.VMEM((peers, 1, 128), f32),
+            pltpu.VMEM((ngx // wide, wide * ngz, 1, 128), f32),
+            pltpu.VMEM((1, 128), f32),
             pltpu.VMEM((1, 128), f32),
             pltpu.VMEM((5, cz, rows), f32),
             pltpu.VMEM((5, cz // 8 + 6, 8, rows), f32),
@@ -425,12 +643,17 @@
             pltpu.VMEM((5, ny + 6, cx, cz), f32),
             pltpu.VMEM((5, ny + 6, cx, cz), f32),
             pltpu.VMEM((max(parts - 1, 1), 5, cx + 6, 8, cz), f32),
+            pltpu.VMEM((max(parts - 1, 1), 11, 5, cx - 2, 8, cz), f32),
+            pltpu.VMEM((11, 5, ny + 4, cx, cz), f32),
+            pltpu.VMEM((11, 5, cz // 8 + 4, 8, rows), f32),
             pltpu.SemaphoreType.DMA,
             pltpu.SemaphoreType.DMA((3,)),
-            pltpu.SemaphoreType.DMA,
-            pltpu.SemaphoreType.DMA,
+            pltpu.SemaphoreType.DMA((ngx // wide,)),
+            pltpu.SemaphoreType.DMA((ngx // wide,)),
             pltpu.SemaphoreType.DMA((2 + 2 * parts,)),
             pltpu.SemaphoreType.DMA((2 + 2 * parts,)),
+            pltpu.SemaphoreType.REGULAR((ngx // wide,)),
+            pltpu.SemaphoreType.REGULAR,
         ],
         compiler_params=pltpu.CompilerParams(collective_id=0, has_side_effects=True),
         name="exchange",
@@ -439,7 +662,7 @@
     return pl.pallas_call(
         functools.partial(update_kernel, cx, ny),
         out_shape=(block, block),
-        in_specs=[inside] * 7,
+        in_specs=[inside] * 8,
         out_specs=(anywhere, anywhere),
         scratch_shapes=[
             pltpu.VMEM((5, cx + 6, 8, cz), f32),

time: 15.3 us -> 14.6 us (0.954)
  Pallas kernels: 14.5 us -> 13.8 us
    pallas_call x1, Pallas kernels: 13.3 us -> 12.6 us  [shards(): pl.pallas_call(functools.partial(exchange_kernel, ngx, ngz, cx, ny), out_...]
where the time goes in v2:
time: 14.6 us; the launch traced here: 14.4 us
  Pallas kernels  13.8 us (95%)
  between operations  0.64 us (4%)
    pallas_call x1, Pallas kernels, shards(): pl.pallas_call(functools.partial(exchange_kernel, ngx, ngz, cx, ny), out_...  12.6 us
    pallas_call x1, Pallas kernels, shards(): pl.pallas_call(functools.partial(update_kernel, cx, ny), out_shape=(block...  1.16 us

profile of v2, /device:TPU:0, one launch (start us, length us, event | category | flops | bytes accessed | tf_op | source)
XLA Modules:
  0.0 14.4 jit_solution(13963093176162550664)
XLA Ops:
  0.6 12.6 %exchange.1 = (f32[5,128,128]{2,1,0:T(8,128)S(1)}, f32[5,224,128]{2,1,0:T(8,128)S(1)}, f32[5,14,8,128]{3,2,1,0:T(8,128)S(1)}, f32[128,128]{1,0:T(8,128)S(1)}, f3...) custom-call(f32[5,128,128]{2,1,0:T(8,128)} %bitcast.6, ...), custom_call_target="tpu_custom_call" | custom-call | tf_op jit(solution)/shard_map/exchange/pallas_call | solution.py:618
  13.2 1.2 %update.1 = (f32[5,8,16,128]{3,2,1,0:T(8,128)}, f32[5,8,16,128]{3,2,1,0:T(8,128)}) custom-call(f32[5,128,128]{2,1,0:T(8,128)S(1)} %get-tuple-element.10.acc, f32[5,224,128]{2,1,0:T(8,128)S(1)} %get-tuple-element.11.xpad, f32[5,14,8,128]{3,2,1,0:T(8,128)S(1)} %get-tuple-element.12.xf_in, f32[128,128]{1,0:T(8,128)S(1)} %get-tuple-element.13.mask, ...), custom_call_target="tpu_custom_call" | custom-call | tf_op jit(solution)/shard_map/update/pallas_call | solution.py:662

commit v3 on v2

--- a/solution.py
+++ b/solution.py
@@ -296,7 +296,7 @@
 def exchange_kernel(
     ngx, ngz, cx, ny, state_ref, register_ref, ghost_ref, flags_ref,
     acc, xpad, xf, mask, top_ref, near, early_register, early_state,
-    zt, reg, ghost, flags, slots, mine, plane_top, acc_t, zf, zu, yf, yu, xf_early, near_early, yq, zq,
+    zt, reg, ghost, flags, slots, mine, plane_top, acc_t, zf, zu, yf, yu, xf_early, near_early, yq, zq, y_base, z_base, y_mask, y_sum,
     load_sem, side_sem, send_sem, recv_sem, halo_send, halo_recv, ready_up, ready_wrap
 ):
     peers = Peers(ngx, ngz)
@@ -411,14 +411,14 @@
         else:
             cons = [ghost[f, y - ny] for f in range(5)]
         store_fluxes(cons, 2, yf, yu, cell)
-    load_register.wait()
+    for cell in range(ny):
+        y_mask[cell] = (LAMBDA[1] / LAMBDA[0]) * mask[pl.ds(cell, 8, stride=ny), :]
 
     def y_linear(f, carry):
         for cell in range(ny):
-            where = pl.ds(cell, 8, stride=ny)
-            weights = difference_weights(mask[where, :] > 0.0)
+            weights = difference_weights(y_mask[cell] > 0.0)
             linear = linear_part(weights, lambda j: yf[f, j + 3], cell)
-            acc[f, where, :] = REGISTER_DECAY * reg[f, where, :] - (LAMBDA[1] / 12.0) * linear
+            y_base[f, cell] = (-LAMBDA[1] / 12.0) * linear
         prepare_line(ny, f, yf, yu, yq)
         return carry
 
@@ -430,6 +430,8 @@
             for field, flux in enumerate(fluxes_of(cons, 1)):
                 target[field, 3 + cell] = flux
 
+    load_register.wait()
+
     def x_linear(f, carry):
         for part in range(parts):
             source = xf if part == parts - 1 else xf_early.at[part]
@@ -446,7 +448,7 @@
                 where = pl.ds(cell * ny + part * 8, 8)
                 weights = difference_weights(mask[where, :] > 0.0)
                 linear = linear_part(weights, inside, cell)
-                acc[f, where, :] = acc[f, where, :] - (LAMBDA[0] / 12.0) * linear
+                acc[f, where, :] = REGISTER_DECAY * reg[f, where, :] - (LAMBDA[0] / 12.0) * linear
         return carry
 
     lax.fori_loop(0, 5, x_linear, 0)
@@ -461,7 +463,7 @@
     def z_linear(f, carry):
         for cell in range(chunk):
             linear = linear_part(weights_t, lambda j: zf[f, j + 3], cell)
-            acc_t[f, pl.ds(cell, 8, stride=chunk), :] = linear
+            z_base[f, cell] = linear
         prepare_line(chunk, f, zf, zu, zq)
         return carry
 
@@ -505,11 +507,11 @@
         for cell in range(chunk):
             after = gap(cell)
             where = pl.ds(cell, 8, stride=chunk)
-            acc_t[f, where, :] = acc_t[f, where, :] - mask_t * (after - before)
+            acc_t[f, where, :] = z_base[f, cell] - mask_t * (after - before)
             before = after
         return carry
 
-    lax.fori_loop(0, 5, z_field, 0)
+    lax.fori_loop(0, 5, z_field, 0, unroll=True)
 
     def y_field(f, carry):
         gap = prepared_gaps(alpha[1], lambda k, j: yq[k, f, j + 2])
@@ -518,29 +520,28 @@
         for cell in range(ny):
             after = gap(cell)
             where = pl.ds(cell, 8, stride=ny)
-            scaled = (LAMBDA[1] / LAMBDA[0]) * mask[where, :]
-            acc[f, where, :] = acc[f, where, :] - scaled * (after - before)
+            y_sum[f, where, :] = y_base[f, cell] - y_mask[cell] * (after - before)
             before = after
         return carry
 
-    lax.fori_loop(0, 5, y_field, 0)
+    lax.fori_loop(0, 5, y_field, 0, unroll=True)
 
     def x_field(f, carry):
         for part in range(parts):
             found = near if part == parts - 1 else near_early.at[part]
             at = lambda cell: pl.ds(cell * ny + part * 8, 8)
             gap = prepared_gaps(alpha[0], lambda k, j: found[k, f, j - 1])
-            for cell in range(2, cx - 2):
-                if cell == 2:
-                    jump = gap(2)
-                elif cell == cx - 3:
-                    jump = -gap(cell - 1)
-                else:
-                    jump = gap(cell) - gap(cell - 1)
-                acc[f, at(cell), :] = acc[f, at(cell), :] - mask[at(cell), :] * jump
+            for cell in range(cx):
+                total = acc[f, at(cell), :] + y_sum[f, at(cell), :]
+                jump = None
+                if 2 <= cell < cx - 3:
+                    jump = gap(cell)
+                if 2 < cell <= cx - 3:
+                    jump = -gap(cell - 1) if jump is None else jump - gap(cell - 1)
+                acc[f, at(cell), :] = total if jump is None else total - mask[at(cell), :] * jump
         return carry
 
-    lax.fori_loop(0, 5, x_field, 0)
+    lax.fori_loop(0, 5, x_field, 0, unroll=True)
 
     for part in range(parts):
         to_left[part].wait()
@@ -558,7 +559,7 @@
                 )
                 return carry
 
-            lax.fori_loop(0, 5, early, 0)
+            lax.fori_loop(0, 5, early, 0, unroll=True)
 
     def departures(plane):
         @pl.when(plane > peers.q)
@@ -646,6 +647,10 @@
             pltpu.VMEM((max(parts - 1, 1), 11, 5, cx - 2, 8, cz), f32),
             pltpu.VMEM((11, 5, ny + 4, cx, cz), f32),
             pltpu.VMEM((11, 5, cz // 8 + 4, 8, rows), f32),
+            pltpu.VMEM((5, ny, cx, cz), f32),
+            pltpu.VMEM((5, cz // 8, 8, rows), f32),
+            pltpu.VMEM((ny, cx, cz), f32),
+            pltpu.VMEM((5, rows, cz), f32),
             pltpu.SemaphoreType.DMA,
             pltpu.SemaphoreType.DMA((3,)),
             pltpu.SemaphoreType.DMA((ngx // wide,)),

time: 14.6 us -> 14 us (0.959)
  Pallas kernels: 13.8 us -> 13.2 us
    pallas_call x1, Pallas kernels: 12.6 us -> 12.1 us  [shards(): pl.pallas_call(functools.partial(exchange_kernel, ngx, ngz, cx, ny), out_...]
where the time goes in v3:
time: 14 us; the launch traced here: 13.9 us
  Pallas kernels  13.2 us (94%)
  between operations  0.64 us (5%)
    pallas_call x1, Pallas kernels, shards(): pl.pallas_call(functools.partial(exchange_kernel, ngx, ngz, cx, ny), out_...  12.1 us
    pallas_call x1, Pallas kernels, shards(): pl.pallas_call(functools.partial(update_kernel, cx, ny), out_shape=(block...  1.16 us

profile of v3, /device:TPU:0, one launch (start us, length us, event | category | flops | bytes accessed | tf_op | source)
XLA Modules:
  0.0 13.9 jit_solution(4440151443275171959)
XLA Ops:
  0.6 12.1 %exchange.1 = (f32[5,128,128]{2,1,0:T(8,128)S(1)}, f32[5,224,128]{2,1,0:T(8,128)S(1)}, f32[5,14,8,128]{3,2,1,0:T(8,128)S(1)}, f32[128,128]{1,0:T(8,128)S(1)}, f3...) custom-call(f32[5,128,128]{2,1,0:T(8,128)} %bitcast.6, ...), custom_call_target="tpu_custom_call" | custom-call | tf_op jit(solution)/shard_map/exchange/pallas_call | solution.py:619
  12.7 1.2 %update.1 = (f32[5,8,16,128]{3,2,1,0:T(8,128)}, f32[5,8,16,128]{3,2,1,0:T(8,128)}) custom-call(f32[5,128,128]{2,1,0:T(8,128)S(1)} %get-tuple-element.10.acc, f32[5,224,128]{2,1,0:T(8,128)S(1)} %get-tuple-element.11.xpad, f32[5,14,8,128]{3,2,1,0:T(8,128)S(1)} %get-tuple-element.12.xf_in, f32[128,128]{1,0:T(8,128)S(1)} %get-tuple-element.13.mask, ...), custom_call_target="tpu_custom_call" | custom-call | tf_op jit(solution)/shard_map/update/pallas_call | solution.py:667

commit v4 on v2

--- a/solution.py
+++ b/solution.py
@@ -165,11 +165,11 @@
                 store(3 * kind + power, j, term)
 
 
-def prepare_third(flux, cons, cells, store):
+def prepare_third(flux, cons, cells, store, scale=1.0):
     f, u = Line(flux), Line(cons)
     for j in cells:
-        store(9, j, f.T(j))
-        store(10, j, u.T(j))
+        store(9, j, f.T(j) if scale == 1.0 else scale * f.T(j))
+        store(10, j, u.T(j) if scale == 1.0 else scale * u.T(j))
 
 
 class Prepared:
@@ -255,48 +255,46 @@
         conserved[field, cell] = cons[field]
 
 
-def prepare_line(count, f, fluxes, conserved, out):
+def prepare_line(count, scale, f, fluxes, conserved, out):
     def keep(kind, j, value):
         out[kind, f, j + 2] = value
 
     flux, cons = cached(lambda j: fluxes[f, j + 3]), cached(lambda j: conserved[f, j + 3])
     prepare(flux, cons, range(-2, count + 2), keep)
-    prepare_third(flux, cons, range(-2, count + 1), keep)
-
-
-def halo_fluxes(cx, ny, part, xpad, xf):
-    for cell in (0, 1, 2, cx + 3, cx + 4, cx + 5):
-        cons = [xpad[f, pl.ds(cell * ny + part * 8, 8), :] for f in range(5)]
+    prepare_third(flux, cons, range(-2, count + 1), keep, scale)
+
+
+def store_x_fluxes(ny, part, cells, xpad, xf):
+    for cell in cells:
+        cons = [xpad[f, pl.ds((cell + 3) * ny + part * 8, 8), :] for f in range(5)]
         for field, flux in enumerate(fluxes_of(cons, 1)):
-            xf[field, cell] = flux
-
-
-def edge_update(cx, ny, part, f, alpha, xpad, xf, mask, acc, near, emit):
+            xf[part, field, cell + 3] = flux
+
+
+def left_edge(ny, part, alpha, xpad, flux, mask, acc, known, jumps, emit):
     rows = lambda cell: pl.ds(cell * ny + part * 8, 8)
-    gap = edge_gaps(
-        alpha, lambda j: xf[f, j + 3], lambda j: xpad[f, rows(j + 3), :],
-        lambda k, j: near[k, f, j - 1], range(1, cx - 1), range(1, cx - 2),
-    )
-    outside = lambda j: xf[f, j + 3] if j < 0 or j >= cx else None
-    for cell in range(cx):
-        total = acc[f, rows(cell), :]
-        if cell < 3 or cell >= cx - 3:
-            scaled = mask[rows(cell), :]
-            weights = difference_weights(scaled > 0.0)
-            missing = linear_part([w * (LAMBDA[0] / 12.0) for w in weights], outside, cell)
-            jump = None
-            if cell < 2 or cell >= cx - 3:
-                jump = gap(cell)
-            if cell < 3 or cell > cx - 3:
-                jump = -gap(cell - 1) if jump is None else jump - gap(cell - 1)
-            total = total - (missing + scaled * jump)
-        emit(cell, total)
+    scaled = [mask[rows(cell), :] for cell in range(3)]
+    weights = [
+        [weight * (LAMBDA[0] / 12.0) for weight in difference_weights(m > 0.0)] for m in scaled
+    ]
+    for f in range(5):
+        gap = edge_gaps(
+            alpha, lambda j: flux(f, j), lambda j: xpad[f, rows(j + 3), :],
+            lambda k, j: known(k, f, j), range(1, 4), range(1, 4),
+        )
+        outside = lambda j: flux(f, j) if j < 0 else None
+        for cell in range(3):
+            jump = jumps[f, rows(cell), :] - gap(cell - 1)
+            if cell < 2:
+                jump = jump + gap(cell)
+            missing = linear_part(weights[cell], outside, cell)
+            emit(f, cell, acc[f, rows(cell), :] - (missing + scaled[cell] * jump))
 
 
 def exchange_kernel(
     ngx, ngz, cx, ny, state_ref, register_ref, ghost_ref, flags_ref,
-    acc, xpad, xf, mask, top_ref, near, early_register, early_state,
-    zt, reg, ghost, flags, slots, mine, plane_top, acc_t, zf, zu, yf, yu, xf_early, near_early, yq, zq,
+    acc, xpad, mask, top_ref, edge_flux, edge_near, jumps, done_register, done_state,
+    zt, reg, ghost, flags, slots, mine, plane_top, acc_t, zf, zu, yf, yu, yq, zq, xf, near,
     load_sem, side_sem, send_sem, recv_sem, halo_send, halo_recv, ready_up, ready_wrap
 ):
     peers = Peers(ngx, ngz)
@@ -309,15 +307,15 @@
     load = pltpu.make_async_copy(state_ref, xpad.at[:, pl.ds(halo, rows), :], load_sem)
     load.start()
     load_flags = pltpu.make_async_copy(flags_ref, flags, side_sem.at[0])
-    load_flags.start()
     load_ghost = pltpu.make_async_copy(ghost_ref, ghost, side_sem.at[1])
-    load_ghost.start()
     load_register = pltpu.make_async_copy(register_ref, reg, side_sem.at[2])
-    load_register.start()
     slots[...] = jnp.zeros(slots.shape, slots.dtype)
     barrier = pltpu.get_barrier_semaphore()
     peers.greet(barrier)
     load.wait()
+    load_flags.start()
+    load_ghost.start()
+    load_register.start()
     best = None
     for row in range(0, rows, 8):
         cons = [xpad[var, pl.ds(halo + row, 8), :] for var in range(5)]
@@ -372,12 +370,18 @@
     each(peers.planes, tell_lower, peers.unroll)
     peers.plane_mates(lambda index, tx, tz: tell(mine, peers.q, peers.own, (tx, tz)))
 
+    yields = peers.last & (gz > 0)
+
     @pl.when(peers.last)
     def _():
-        start(to_right)
         signal(ready_wrap, (0, gz))
-
-    @pl.when(gx > 0)
+        start(to_right[:1])
+
+    @pl.when(peers.last & (gz == 0))
+    def _():
+        start(to_right[1:])
+
+    @pl.when((gx > 0) & jnp.logical_not(yields))
     def _():
         start(to_left)
 
@@ -419,37 +423,61 @@
             weights = difference_weights(mask[where, :] > 0.0)
             linear = linear_part(weights, lambda j: yf[f, j + 3], cell)
             acc[f, where, :] = REGISTER_DECAY * reg[f, where, :] - (LAMBDA[1] / 12.0) * linear
-        prepare_line(ny, f, yf, yu, yq)
+        prepare_line(ny, LAMBDA[1] / LAMBDA[0], f, yf, yu, yq)
         return carry
 
     lax.fori_loop(0, 5, y_linear, 0)
+
+    @pl.when(yields)
+    def _():
+        start(to_right[1:])
+        start(to_left)
+
     for part in range(parts):
-        target = xf if part == parts - 1 else xf_early.at[part]
-        for cell in range(cx):
-            cons = [xpad[f, pl.ds(halo + cell * ny + part * 8, 8), :] for f in range(5)]
-            for field, flux in enumerate(fluxes_of(cons, 1)):
-                target[field, 3 + cell] = flux
-
-    def x_linear(f, carry):
+        store_x_fluxes(ny, part, range(cx), xpad, xf)
+
+    def x_prepare(f, part, centres, thirds):
+        def keep(kind, j, value):
+            near[part, kind, f, j - 1] = value
+
+        flux = cached(lambda j: xf[part, f, j + 3])
+        cons = cached(lambda j: xpad[f, pl.ds((j + 3) * ny + part * 8, 8), :])
+        prepare(flux, cons, centres, keep)
+        prepare_third(flux, cons, thirds, keep)
+
+    def x_linear(f, part, cells, known):
+        for cell in cells:
+            where = pl.ds(cell * ny + part * 8, 8)
+            weights = difference_weights(mask[where, :] > 0.0)
+            linear = linear_part(weights, lambda j: xf[part, f, j + 3] if known(j) else None, cell)
+            acc[f, where, :] = acc[f, where, :] - (LAMBDA[0] / 12.0) * linear
+
+    def x_inner(f, carry):
         for part in range(parts):
-            source = xf if part == parts - 1 else xf_early.at[part]
-            found = near if part == parts - 1 else near_early.at[part]
-            inside = lambda j: source[f, j + 3] if 0 <= j < cx else None
-
-            def keep(kind, j, value):
-                found[kind, f, j - 1] = value
-
-            at = lambda j: pl.ds((j + 3) * ny + part * 8, 8)
-            prepare(inside, lambda j: xpad[f, at(j), :], range(1, cx - 1), keep)
-            prepare_third(inside, lambda j: xpad[f, at(j), :], range(1, cx - 2), keep)
-            for cell in range(cx):
-                where = pl.ds(cell * ny + part * 8, 8)
-                weights = difference_weights(mask[where, :] > 0.0)
-                linear = linear_part(weights, inside, cell)
-                acc[f, where, :] = acc[f, where, :] - (LAMBDA[0] / 12.0) * linear
+            x_prepare(f, part, range(1, cx - 1), range(1, cx - 2))
+            if part == parts - 1:
+                for cell in range(5):
+                    edge_flux[f, cell] = xf[part, f, cell + 3]
+                for kind in range(11):
+                    for j in range(1, 4):
+                        edge_near[kind, f, j - 1] = near[part, kind, f, j - 1]
+            x_linear(f, part, range(cx), lambda j: 0 <= j < cx)
         return carry
 
-    lax.fori_loop(0, 5, x_linear, 0)
+    lax.fori_loop(0, 5, x_inner, 0)
+
+    def right_edge():
+        for part in range(parts):
+            to_left[part].wait_recv()
+            store_x_fluxes(ny, part, range(cx, cx + 3), xpad, xf)
+
+        def field(f, carry):
+            for part in range(parts):
+                x_prepare(f, part, range(cx - 1, cx + 2), range(cx - 2, cx + 1))
+                x_linear(f, part, range(cx - 3, cx), lambda j: j >= cx)
+            return carry
+
+        lax.fori_loop(0, 5, field, 0)
 
     for copy in z_copies:
         copy.wait()
@@ -462,7 +490,8 @@
         for cell in range(chunk):
             linear = linear_part(weights_t, lambda j: zf[f, j + 3], cell)
             acc_t[f, pl.ds(cell, 8, stride=chunk), :] = linear
-        prepare_line(chunk, f, zf, zu, zq)
+        acc[f] = acc[f] + acc_t[f].T
+        prepare_line(chunk, LAMBDA[2] / LAMBDA[0], f, zf, zu, zq)
         return carry
 
     lax.fori_loop(0, 5, z_linear, 0)
@@ -484,6 +513,10 @@
     def _():
         pl.semaphore_wait(ready_wrap, 1)
         start(to_left)
+
+    @pl.when(jnp.logical_not(peers.last))
+    def _():
+        right_edge()
 
     def arrivals(plane):
         @pl.when(plane > peers.q)
@@ -504,61 +537,60 @@
         before = gap(-1)
         for cell in range(chunk):
             after = gap(cell)
-            where = pl.ds(cell, 8, stride=chunk)
-            acc_t[f, where, :] = acc_t[f, where, :] - mask_t * (after - before)
+            acc_t[f, pl.ds(cell, 8, stride=chunk), :] = after - before
             before = after
         return carry
 
-    lax.fori_loop(0, 5, z_field, 0)
+    lax.fori_loop(0, 5, z_field, 0, unroll=True)
 
     def y_field(f, carry):
         gap = prepared_gaps(alpha[1], lambda k, j: yq[k, f, j + 2])
-        acc[f] = acc[f] + acc_t[f].T
         before = gap(-1)
         for cell in range(ny):
             after = gap(cell)
-            where = pl.ds(cell, 8, stride=ny)
-            scaled = (LAMBDA[1] / LAMBDA[0]) * mask[where, :]
-            acc[f, where, :] = acc[f, where, :] - scaled * (after - before)
+            jumps[f, pl.ds(cell, 8, stride=ny), :] = after - before
             before = after
         return carry
 
-    lax.fori_loop(0, 5, y_field, 0)
+    lax.fori_loop(0, 5, y_field, 0, unroll=True)
+
+    @pl.when(peers.last)
+    def _():
+        right_edge()
+
+    def finish(part, f, cell, total):
+        done_register[part, f, cell] = total
+        state = xpad[f, pl.ds((cell + 3) * ny + part * 8, 8), :]
+        done_state[part, f, cell] = state + UPDATE_WEIGHT * total
 
     def x_field(f, carry):
+        turned = acc_t[f].T
         for part in range(parts):
-            found = near if part == parts - 1 else near_early.at[part]
-            at = lambda cell: pl.ds(cell * ny + part * 8, 8)
-            gap = prepared_gaps(alpha[0], lambda k, j: found[k, f, j - 1])
-            for cell in range(2, cx - 2):
-                if cell == 2:
-                    jump = gap(2)
-                elif cell == cx - 3:
-                    jump = -gap(cell - 1)
+            gap = prepared_gaps(alpha[0], lambda k, j: near[part, k, f, j - 1])
+            for cell in range(cx):
+                first = cell * ny + part * 8
+                where = pl.ds(first, 8)
+                jump = jumps[f, where, :] + turned[first : first + 8]
+                if cell >= 2:
+                    jump = jump + gap(cell)
+                if cell >= 3:
+                    finish(part, f, cell, acc[f, where, :] - mask[where, :] * (jump - gap(cell - 1)))
                 else:
-                    jump = gap(cell) - gap(cell - 1)
-                acc[f, at(cell), :] = acc[f, at(cell), :] - mask[at(cell), :] * jump
+                    jumps[f, where, :] = jump
         return carry
 
-    lax.fori_loop(0, 5, x_field, 0)
+    lax.fori_loop(0, 5, x_field, 0, unroll=True)
 
     for part in range(parts):
-        to_left[part].wait()
-        to_right[part].wait()
+        to_right[part].wait_recv()
         if part < parts - 1:
-            halo_fluxes(cx, ny, part, xpad, xf_early.at[part])
-
-            def early(f, carry):
-                def emit(cell, total):
-                    state = xpad[f, pl.ds(halo + cell * ny + part * 8, 8), :]
-                    early_register[part, f, cell] = total
-                    early_state[part, f, cell] = state + UPDATE_WEIGHT * total
-                edge_update(
-                    cx, ny, part, f, alpha[0], xpad, xf_early.at[part], mask, acc, near_early.at[part], emit
-                )
-                return carry
-
-            lax.fori_loop(0, 5, early, 0)
+            store_x_fluxes(ny, part, range(-3, 0), xpad, xf)
+            flux = lambda f, j: xf[part, f, j + 3]
+            known = lambda k, f, j: near[part, k, f, j - 1]
+            emit = functools.partial(finish, part)
+            left_edge(ny, part, alpha[0], xpad, flux, mask, acc, known, jumps, emit)
+    for copy in to_left + to_right:
+        copy.wait_send()
 
     def departures(plane):
         @pl.when(plane > peers.q)
@@ -574,11 +606,10 @@
 
 
 def update_kernel(
-    cx, ny, acc, xpad, xf_in, mask, top_ref, near, early_register, early_state,
-    state_out, register_out, xf, late_register, late_state, sems
+    cx, ny, acc, xpad, mask, top_ref, edge_flux, edge_near, jumps, done_register, done_state,
+    state_out, register_out, late_register, late_state, sems
 ):
-    parts = ny // 8
-    part = parts - 1
+    last = ny // 8 - 1
     copies = []
 
     def put(src, dst):
@@ -586,22 +617,29 @@
         copy.start()
         copies.append(copy)
 
-    for p in range(parts - 1):
-        put(early_register.at[p], register_out.at[:, :, pl.ds(p * 8, 8), :])
-        put(early_state.at[p], state_out.at[:, :, pl.ds(p * 8, 8), :])
-    halo_fluxes(cx, ny, part, xpad, xf)
-    for f in range(5):
-        for cell in range(3, cx + 3):
-            xf[f, cell] = xf_in[f, cell]
+    for part in range(last + 1):
+        first = 3 if part == last else 0
+        block = pl.ds(first, cx - first)
+        rows = pl.ds(part * 8, 8)
+        put(done_register.at[part, :, block], register_out.at[:, block, rows, :])
+        put(done_state.at[part, :, block], state_out.at[:, block, rows, :])
+    halo = [
+        fluxes_of([xpad[f, pl.ds((3 + cell) * ny + last * 8, 8), :] for f in range(5)], 1)
+        for cell in range(-3, 0)
+    ]
+
+    def emit(f, cell, total):
+        state = xpad[f, pl.ds((3 + cell) * ny + last * 8, 8), :]
+        late_register[f, cell] = total
+        late_state[f, cell] = state + UPDATE_WEIGHT * total
+
     alpha = jnp.broadcast_to(top_ref[:, 0:1], (8, 128))
-    for f in range(5):
-        def emit(cell, total):
-            state = xpad[f, pl.ds((3 + cell) * ny + part * 8, 8), :]
-            late_register[f, cell] = total
-            late_state[f, cell] = state + UPDATE_WEIGHT * total
-        edge_update(cx, ny, part, f, alpha, xpad, xf, mask, acc, near, emit)
-        put(late_register.at[f], register_out.at[f, :, pl.ds(part * 8, 8), :])
-        put(late_state.at[f], state_out.at[f, :, pl.ds(part * 8, 8), :])
+    flux = lambda f, j: halo[j + 3][f] if j < 0 else edge_flux[f, j]
+    known = lambda k, f, j: edge_near[k, f, j - 1]
+    left_edge(ny, last, alpha, xpad, flux, mask, acc, known, jumps, emit)
+    block, rows = pl.ds(0, 3), pl.ds(last * 8, 8)
+    put(late_register, register_out.at[:, block, rows, :])
+    put(late_state, state_out.at[:, block, rows, :])
     for copy in copies:
         copy.wait()
 
@@ -620,15 +658,16 @@
         out_shape=(
             pltpu.VMEM((5, rows, cz), f32),
             pltpu.VMEM((5, (cx + 6) * ny, cz), f32),
-            pltpu.VMEM((5, cx + 6, 8, cz), f32),
             pltpu.VMEM((rows, cz), f32),
             pltpu.VMEM((8, 128), f32),
-            pltpu.VMEM((11, 5, cx - 2, 8, cz), f32),
-            pltpu.VMEM((max(parts - 1, 1), 5, cx, 8, cz), f32),
-            pltpu.VMEM((max(parts - 1, 1), 5, cx, 8, cz), f32),
+            pltpu.VMEM((5, 5, 8, cz), f32),
+            pltpu.VMEM((11, 5, 3, 8, cz), f32),
+            pltpu.VMEM((5, rows, cz), f32),
+            pltpu.VMEM((parts, 5, cx, 8, cz), f32),
+            pltpu.VMEM((parts, 5, cx, 8, cz), f32),
         ),
         in_specs=[anywhere] * 4,
-        out_specs=(inside,) * 8,
+        out_specs=(inside,) * 9,
         scratch_shapes=[
             pltpu.VMEM((5, cz + 16, rows), f32),
             pltpu.VMEM((5, rows, cz), f32),
@@ -642,10 +681,10 @@
             pltpu.VMEM((5, cz // 8 + 6, 8, rows), f32),
             pltpu.VMEM((5, ny + 6, cx, cz), f32),
             pltpu.VMEM((5, ny + 6, cx, cz), f32),
-            pltpu.VMEM((max(parts - 1, 1), 5, cx + 6, 8, cz), f32),
-            pltpu.VMEM((max(parts - 1, 1), 11, 5, cx - 2, 8, cz), f32),
             pltpu.VMEM((11, 5, ny + 4, cx, cz), f32),
             pltpu.VMEM((11, 5, cz // 8 + 4, 8, rows), f32),
+            pltpu.VMEM((parts, 5, cx + 6, 8, cz), f32),
+            pltpu.VMEM((parts, 11, 5, cx + 1, 8, cz), f32),
             pltpu.SemaphoreType.DMA,
             pltpu.SemaphoreType.DMA((3,)),
             pltpu.SemaphoreType.DMA((ngx // wide,)),
@@ -662,13 +701,12 @@
     return pl.pallas_call(
         functools.partial(update_kernel, cx, ny),
         out_shape=(block, block),
-        in_specs=[inside] * 8,
+        in_specs=[inside] * 9,
         out_specs=(anywhere, anywhere),
         scratch_shapes=[
-            pltpu.VMEM((5, cx + 6, 8, cz), f32),
-            pltpu.VMEM((5, cx, 8, cz), f32),
-            pltpu.VMEM((5, cx, 8, cz), f32),
-            pltpu.SemaphoreType.DMA((2 * (parts - 1) + 10,)),
+            pltpu.VMEM((5, 3, 8, cz), f32),
+            pltpu.VMEM((5, 3, 8, cz), f32),
+            pltpu.SemaphoreType.DMA((2 * parts + 2,)),
         ],
         name="update",
     )(*(pltpu.with_memory_space_constraint(array, pltpu.VMEM) for array in held))

time: 14.6 us -> 13.7 us (0.938)
  Pallas kernels: 13.8 us -> 12.9 us
    pallas_call x1, Pallas kernels: 12.6 us -> 11.9 us  [shards(): pl.pallas_call(functools.partial(exchange_kernel, ngx, ngz, cx, ny), out_...]
    pallas_call x1, Pallas kernels: 1.16 us -> 0.96 us  [shards(): pl.pallas_call(functools.partial(update_kernel, cx, ny), out_shape=(block...]
where the time goes in v4:
time: 13.7 us; the launch traced here: 13.5 us
  Pallas kernels  12.9 us (94%)
  between operations  0.64 us (5%)
    pallas_call x1, Pallas kernels, shards(): pl.pallas_call(functools.partial(exchange_kernel, ngx, ngz, cx, ny), out_...  11.9 us
    pallas_call x1, Pallas kernels, shards(): pl.pallas_call(functools.partial(update_kernel, cx, ny), out_shape=(block...  0.96 us

profile of v4, /device:TPU:0, one launch (start us, length us, event | category | flops | bytes accessed | tf_op | source)
XLA Modules:
  0.0 13.5 jit_solution(6229477783300897426)
XLA Ops:
  0.6 11.9 %exchange.1 = (f32[5,128,128]{2,1,0:T(8,128)S(1)}, f32[5,224,128]{2,1,0:T(8,128)S(1)}, f32[128,128]{1,0:T(8,128)S(1)}, f32[8,128]{1,0:T(8,128)S(1)}, f32[5,5,8,1...) custom-call(f32[5,128,128]{2,1,0:T(8,128)} %bitcast.6, ...), custom_call_target="tpu_custom_call" | custom-call | tf_op jit(solution)/shard_map/exchange/pallas_call | solution.py:656
  12.5 1.0 %update.1 = (f32[5,8,16,128]{3,2,1,0:T(8,128)}, f32[5,8,16,128]{3,2,1,0:T(8,128)}) custom-call(f32[5,128,128]{2,1,0:T(8,128)S(1)} %get-tuple-element.11.acc, f32[5,224,128]{2,1,0:T(8,128)S(1)} %get-tuple-element.12.xpad, f32[128,128]{1,0:T(8,128)S(1)} %get-tuple-element.13.mask, f32[8,128]{1,0:T(8,128)S(1)} %get-tuple-element.14.top_ref, ...), custom_call_target="tpu_custom_call" | custom-call | tf_op jit(solution)/shard_map/update/pallas_call | solution.py:701

commit v5 on v4

--- a/solution.py
+++ b/solution.py
@@ -308,7 +308,7 @@
     load.start()
     load_flags = pltpu.make_async_copy(flags_ref, flags, side_sem.at[0])
     load_ghost = pltpu.make_async_copy(ghost_ref, ghost, side_sem.at[1])
-    load_register = pltpu.make_async_copy(register_ref, reg, side_sem.at[2])
+    load_register = pltpu.make_async_copy(register_ref, reg, load_sem)
     slots[...] = jnp.zeros(slots.shape, slots.dtype)
     barrier = pltpu.get_barrier_semaphore()
     peers.greet(barrier)
@@ -330,18 +330,21 @@
     right, left = shifted(gx, 1, ngx), shifted(gx, ngx - 1, ngx)
     high, low = shifted(gz, 1, ngz), shifted(gz, ngz - 1, ngz)
 
-    def move(index, src, dst, target):
+    def move(leaves, comes, src, dst, target):
         return pltpu.make_async_remote_copy(
-            src_ref=src, dst_ref=dst, send_sem=halo_send.at[index], recv_sem=halo_recv.at[index],
+            src_ref=src, dst_ref=dst, send_sem=halo_send.at[leaves], recv_sem=halo_recv.at[comes],
             device_id=target, device_id_type=MESH,
         )
+
+    def all_bytes(some, semaphore):
+        pltpu.make_async_copy(some, some, semaphore).wait()
 
     blocks = xpad.reshape(5, cx + 6, ny, xpad.shape[2])
     to_left, to_right = [], []
     for part in range(parts):
         layers = lambda first: blocks.at[:, pl.ds(first, 3), pl.ds(part * 8, 8), :]
-        to_left.append(move(2 + 2 * part, layers(3), layers(3 + cx), (left, gz)))
-        to_right.append(move(3 + 2 * part, layers(cx), layers(0), (right, gz)))
+        to_left.append(move(1, 1, layers(3), layers(3 + cx), (left, gz)))
+        to_right.append(move(1, 2 + part, layers(cx), layers(0), (right, gz)))
 
     def start(copies):
         for copy in copies:
@@ -350,10 +353,10 @@
     def signal(semaphore, target):
         pl.semaphore_signal(semaphore, inc=1, device_id=target, device_id_type=MESH)
 
-    def tell(source, plane, index, target):
+    def tell(source, far, index, target):
         pltpu.make_async_remote_copy(
-            src_ref=source, dst_ref=slots.at[peers.q, index], send_sem=send_sem.at[plane],
-            recv_sem=recv_sem.at[peers.q], device_id=target, device_id_type=MESH,
+            src_ref=source, dst_ref=slots.at[peers.q, index], send_sem=send_sem,
+            recv_sem=recv_sem.at[far], device_id=target, device_id_type=MESH,
         ).start()
 
     pl.semaphore_wait(barrier, peers.greetings())
@@ -363,12 +366,12 @@
         def _():
             each(
                 peers.members,
-                lambda index: tell(mine, plane, peers.own, peers.member(plane, index)),
+                lambda index: tell(mine, 1, peers.own, peers.member(plane, index)),
                 peers.unroll,
             )
 
     each(peers.planes, tell_lower, peers.unroll)
-    peers.plane_mates(lambda index, tx, tz: tell(mine, peers.q, peers.own, (tx, tz)))
+    peers.plane_mates(lambda index, tx, tz: tell(mine, 0, peers.own, (tx, tz)))
 
     yields = peers.last & (gz > 0)
 
@@ -389,12 +392,12 @@
     def _():
         start(to_right)
 
-    peers.columns(lambda plane: plane < peers.q, lambda plane, target: signal(ready_up.at[peers.q], target))
+    peers.columns(lambda plane: plane < peers.q, lambda plane, target: signal(ready_up, target))
     for var in range(5):
         zt[var, pl.ds(8, strip), :] = xpad[var, pl.ds(halo, rows), :].T
     z_copies = [
-        move(0, zt.at[:, pl.ds(8, 8), :], zt.at[:, pl.ds(8 + strip, 8), :], (gx, low)),
-        move(1, zt.at[:, pl.ds(strip, 8), :], zt.at[:, pl.ds(0, 8), :], (gx, high)),
+        move(0, 0, zt.at[:, pl.ds(8, 8), :], zt.at[:, pl.ds(8 + strip, 8), :], (gx, low)),
+        move(0, 0, zt.at[:, pl.ds(strip, 8), :], zt.at[:, pl.ds(0, 8), :], (gx, high)),
     ]
     start(z_copies)
     load_flags.wait()
@@ -467,8 +470,8 @@
     lax.fori_loop(0, 5, x_inner, 0)
 
     def right_edge():
+        all_bytes(xpad.at[:, pl.ds(0, halo), :], halo_recv.at[1])
         for part in range(parts):
-            to_left[part].wait_recv()
             store_x_fluxes(ny, part, range(cx, cx + 3), xpad, xf)
 
         def field(f, carry):
@@ -479,8 +482,8 @@
 
         lax.fori_loop(0, 5, field, 0)
 
-    for copy in z_copies:
-        copy.wait()
+    all_bytes(zt.at[:, pl.ds(0, 16), :], halo_send.at[0])
+    all_bytes(zt.at[:, pl.ds(0, 16), :], halo_recv.at[0])
     for cell in range(chunk + 6):
         cons = [zt[f, pl.ds(5 + cell, 8, stride=chunk), :] for f in range(5)]
         store_fluxes(cons, 3, zf, zu, cell)
@@ -496,18 +499,27 @@
 
     lax.fori_loop(0, 5, z_linear, 0)
 
-    def all_of(plane, count, semaphores):
-        some = slots.at[plane, pl.ds(0, count)]
-        pltpu.make_async_copy(some, some, semaphores.at[plane]).wait()
-
-    all_of(peers.q, peers.members - 1, recv_sem)
+    messages = slots.reshape(peers.planes * peers.members, 1, 128)
+
+    def by_plane(count, semaphore):
+        def visit(plane):
+            number = count(plane)
+            if number:
+                @pl.when(peers.q == plane)
+                def _():
+                    all_bytes(messages.at[pl.ds(0, number)], semaphore)
+
+        for plane in range(peers.planes):
+            visit(plane)
+
+    all_bytes(messages.at[pl.ds(0, peers.members - 1)], recv_sem.at[0])
     plane_top[...] = jnp.maximum(jnp.max(slots[peers.q], axis=0), mine[...])
 
-    def tell_higher(plane, target):
-        pl.semaphore_wait(ready_up.at[plane], 1)
-        tell(plane_top, plane, 0, target)
-
-    peers.columns(lambda plane: plane > peers.q, tell_higher)
+    @pl.when(peers.q < peers.planes - 1)
+    def _():
+        pl.semaphore_wait(ready_up, peers.planes - 1 - peers.q)
+
+    peers.columns(lambda plane: plane > peers.q, lambda plane, target: tell(plane_top, 1, 0, target))
 
     @pl.when(gx == 0)
     def _():
@@ -518,16 +530,7 @@
     def _():
         right_edge()
 
-    def arrivals(plane):
-        @pl.when(plane > peers.q)
-        def _():
-            all_of(plane, peers.members, recv_sem)
-
-        @pl.when(plane < peers.q)
-        def _():
-            all_of(plane, 1, recv_sem)
-
-    each(peers.planes, arrivals, peers.unroll)
+    by_plane(lambda plane: (peers.planes - 1 - plane) * peers.members + plane, recv_sem.at[1])
     top = jnp.maximum(jnp.max(jnp.max(slots[...], axis=0), axis=0), mine[...])
     top_ref[...] = jnp.broadcast_to(top, (8, 128))
     alpha = [jnp.broadcast_to(top[:, k : k + 1], (8, 128)) for k in range(3)]
@@ -543,16 +546,16 @@
 
     lax.fori_loop(0, 5, z_field, 0, unroll=True)
 
-    def y_field(f, carry):
+    def y_field(f):
         gap = prepared_gaps(alpha[1], lambda k, j: yq[k, f, j + 2])
-        before = gap(-1)
+        before = gap(-1) if f == 2 else None
         for cell in range(ny):
             after = gap(cell)
-            jumps[f, pl.ds(cell, 8, stride=ny), :] = after - before
+            jumps[f, pl.ds(cell, 8, stride=ny), :] = after if before is None else after - before
             before = after
-        return carry
-
-    lax.fori_loop(0, 5, y_field, 0, unroll=True)
+
+    for f in range(5):
+        y_field(f)
 
     @pl.when(peers.last)
     def _():
@@ -589,20 +592,9 @@
             known = lambda k, f, j: near[part, k, f, j - 1]
             emit = functools.partial(finish, part)
             left_edge(ny, part, alpha[0], xpad, flux, mask, acc, known, jumps, emit)
-    for copy in to_left + to_right:
-        copy.wait_send()
-
-    def departures(plane):
-        @pl.when(plane > peers.q)
-        def _():
-            all_of(plane, 1, send_sem)
-
-        @pl.when(plane < peers.q)
-        def _():
-            all_of(plane, peers.members, send_sem)
-
-    each(peers.planes, departures, peers.unroll)
-    all_of(peers.q, peers.members - 1, send_sem)
+    all_bytes(xpad.at[:, pl.ds(0, 2 * halo), :], halo_send.at[1])
+
+    by_plane(lambda plane: (plane + 1) * peers.members - 1 + peers.planes - 1 - plane, send_sem)
 
 
 def update_kernel(
@@ -610,19 +602,16 @@
     state_out, register_out, late_register, late_state, sems
 ):
     last = ny // 8 - 1
-    copies = []
-
-    def put(src, dst):
-        copy = pltpu.make_async_copy(src, dst, sems.at[len(copies)])
-        copy.start()
-        copies.append(copy)
+
+    def put(src, dst, which):
+        pltpu.make_async_copy(src, dst, sems.at[which]).start()
 
     for part in range(last + 1):
         first = 3 if part == last else 0
         block = pl.ds(first, cx - first)
         rows = pl.ds(part * 8, 8)
-        put(done_register.at[part, :, block], register_out.at[:, block, rows, :])
-        put(done_state.at[part, :, block], state_out.at[:, block, rows, :])
+        put(done_register.at[part, :, block], register_out.at[:, block, rows, :], 0)
+        put(done_state.at[part, :, block], state_out.at[:, block, rows, :], 1)
     halo = [
         fluxes_of([xpad[f, pl.ds((3 + cell) * ny + last * 8, 8), :] for f in range(5)], 1)
         for cell in range(-3, 0)
@@ -638,10 +627,10 @@
     known = lambda k, f, j: edge_near[k, f, j - 1]
     left_edge(ny, last, alpha, xpad, flux, mask, acc, known, jumps, emit)
     block, rows = pl.ds(0, 3), pl.ds(last * 8, 8)
-    put(late_register, register_out.at[:, block, rows, :])
-    put(late_state, state_out.at[:, block, rows, :])
-    for copy in copies:
-        copy.wait()
+    put(late_register, register_out.at[:, block, rows, :], 0)
+    put(late_state, state_out.at[:, block, rows, :], 1)
+    for which, out in enumerate((register_out, state_out)):
+        pltpu.make_async_copy(out, out, sems.at[which]).wait()
 
 
 def shards(ngx, ngz, state, register, top_ghost, flags):
@@ -686,12 +675,12 @@
             pltpu.VMEM((parts, 5, cx + 6, 8, cz), f32),
             pltpu.VMEM((parts, 11, 5, cx + 1, 8, cz), f32),
             pltpu.SemaphoreType.DMA,
-            pltpu.SemaphoreType.DMA((3,)),
-            pltpu.SemaphoreType.DMA((ngx // wide,)),
-            pltpu.SemaphoreType.DMA((ngx // wide,)),
-            pltpu.SemaphoreType.DMA((2 + 2 * parts,)),
-            pltpu.SemaphoreType.DMA((2 + 2 * parts,)),
-            pltpu.SemaphoreType.REGULAR((ngx // wide,)),
+            pltpu.SemaphoreType.DMA((2,)),
+            pltpu.SemaphoreType.DMA,
+            pltpu.SemaphoreType.DMA((2,)),
+            pltpu.SemaphoreType.DMA((2,)),
+            pltpu.SemaphoreType.DMA((2 + parts,)),
+            pltpu.SemaphoreType.REGULAR,
             pltpu.SemaphoreType.REGULAR,
         ],
         compiler_params=pltpu.CompilerParams(collective_id=0, has_side_effects=True),
@@ -706,7 +695,7 @@
         scratch_shapes=[
             pltpu.VMEM((5, 3, 8, cz), f32),
             pltpu.VMEM((5, 3, 8, cz), f32),
-            pltpu.SemaphoreType.DMA((2 * parts + 2,)),
+            pltpu.SemaphoreType.DMA((2,)),
         ],
         name="update",
     )(*(pltpu.with_memory_space_constraint(array, pltpu.VMEM) for array in held))

time: 13.7 us -> 13.5 us (0.985)
  Pallas kernels: 12.9 us -> 12.7 us
    pallas_call x1, Pallas kernels: 11.9 us -> 11.7 us  [shards(): pl.pallas_call(functools.partial(exchange_kernel, ngx, ngz, cx, ny), out_...]
where the time goes in v5:
time: 13.5 us; the launch traced here: 13.3 us
  Pallas kernels  12.7 us (94%)
  between operations  0.64 us (5%)
    pallas_call x1, Pallas kernels, shards(): pl.pallas_call(functools.partial(exchange_kernel, ngx, ngz, cx, ny), out_...  11.7 us
    pallas_call x1, Pallas kernels, shards(): pl.pallas_call(functools.partial(update_kernel, cx, ny), out_shape=(block...  0.93 us

profile of v5, /device:TPU:0, one launch (start us, length us, event | category | flops | bytes accessed | tf_op | source)
XLA Modules:
  0.0 13.3 jit_solution(4170263160287954974)
XLA Ops:
  0.6 11.7 %exchange.1 = (f32[5,128,128]{2,1,0:T(8,128)S(1)}, f32[5,224,128]{2,1,0:T(8,128)S(1)}, f32[128,128]{1,0:T(8,128)S(1)}, f32[8,128]{1,0:T(8,128)S(1)}, f32[5,5,8,1...) custom-call(f32[5,128,128]{2,1,0:T(8,128)} %bitcast.6, ...), custom_call_target="tpu_custom_call" | custom-call | tf_op jit(solution)/shard_map/exchange/pallas_call | solution.py:645
  12.4 0.9 %update.1 = (f32[5,8,16,128]{3,2,1,0:T(8,128)}, f32[5,8,16,128]{3,2,1,0:T(8,128)}) custom-call(f32[5,128,128]{2,1,0:T(8,128)S(1)} %get-tuple-element.11.acc, f32[5,224,128]{2,1,0:T(8,128)S(1)} %get-tuple-element.12.xpad, f32[128,128]{1,0:T(8,128)S(1)} %get-tuple-element.13.mask, f32[8,128]{1,0:T(8,128)S(1)} %get-tuple-element.14.top_ref, ...), custom_call_target="tpu_custom_call" | custom-call | tf_op jit(solution)/shard_map/update/pallas_call | solution.py:690

commit v6 on v5

--- a/solution.py
+++ b/solution.py
@@ -293,7 +293,7 @@
 
 def exchange_kernel(
     ngx, ngz, cx, ny, state_ref, register_ref, ghost_ref, flags_ref,
-    acc, xpad, mask, top_ref, edge_flux, edge_near, jumps, done_register, done_state,
+    acc, xpad, mask, first_alpha, edge_flux, edge_near, jumps, done_register, done_state,
     zt, reg, ghost, flags, slots, mine, plane_top, acc_t, zf, zu, yf, yu, yq, zq, xf, near,
     load_sem, side_sem, send_sem, recv_sem, halo_send, halo_recv, ready_up, ready_wrap
 ):
@@ -532,8 +532,8 @@
 
     by_plane(lambda plane: (peers.planes - 1 - plane) * peers.members + plane, recv_sem.at[1])
     top = jnp.maximum(jnp.max(jnp.max(slots[...], axis=0), axis=0), mine[...])
-    top_ref[...] = jnp.broadcast_to(top, (8, 128))
     alpha = [jnp.broadcast_to(top[:, k : k + 1], (8, 128)) for k in range(3)]
+    first_alpha[...] = alpha[0]
 
     def z_field(f, carry):
         gap = prepared_gaps(alpha[2], lambda k, j: zq[k, f, j + 2])
@@ -585,6 +585,9 @@
     lax.fori_loop(0, 5, x_field, 0, unroll=True)
 
     for part in range(parts):
+        if part == parts - 1:
+            all_bytes(xpad.at[:, pl.ds(0, 2 * halo), :], halo_send.at[1])
+            by_plane(lambda plane: (plane + 1) * peers.members - 1 + peers.planes - 1 - plane, send_sem)
         to_right[part].wait_recv()
         if part < parts - 1:
             store_x_fluxes(ny, part, range(-3, 0), xpad, xf)
@@ -592,13 +595,10 @@
             known = lambda k, f, j: near[part, k, f, j - 1]
             emit = functools.partial(finish, part)
             left_edge(ny, part, alpha[0], xpad, flux, mask, acc, known, jumps, emit)
-    all_bytes(xpad.at[:, pl.ds(0, 2 * halo), :], halo_send.at[1])
-
-    by_plane(lambda plane: (plane + 1) * peers.members - 1 + peers.planes - 1 - plane, send_sem)
 
 
 def update_kernel(
-    cx, ny, acc, xpad, mask, top_ref, edge_flux, edge_near, jumps, done_register, done_state,
+    cx, ny, acc, xpad, mask, first_alpha, edge_flux, edge_near, jumps, done_register, done_state,
     state_out, register_out, late_register, late_state, sems
 ):
     last = ny // 8 - 1
@@ -622,7 +622,7 @@
         late_register[f, cell] = total
         late_state[f, cell] = state + UPDATE_WEIGHT * total
 
-    alpha = jnp.broadcast_to(top_ref[:, 0:1], (8, 128))
+    alpha = first_alpha[...]
     flux = lambda f, j: halo[j + 3][f] if j < 0 else edge_flux[f, j]
     known = lambda k, f, j: edge_near[k, f, j - 1]
     left_edge(ny, last, alpha, xpad, flux, mask, acc, known, jumps, emit)

time: 13.5 us -> 13.4 us (level)
  no operation moved by 1% of the time
where the time goes in v6:
time: 13.4 us; the launch traced here: 13.2 us
  Pallas kernels  12.6 us (94%)
  between operations  0.64 us (5%)
    pallas_call x1, Pallas kernels, shards(): pl.pallas_call(functools.partial(exchange_kernel, ngx, ngz, cx, ny), out_...  11.7 us
    pallas_call x1, Pallas kernels, shards(): pl.pallas_call(functools.partial(update_kernel, cx, ny), out_shape=(block...  0.87 us

profile of v6, /device:TPU:0, one launch (start us, length us, event | category | flops | bytes accessed | tf_op | source)
XLA Modules:
  0.0 13.2 jit_solution(13523235349870052281)
XLA Ops:
  0.6 11.7 %exchange.1 = (f32[5,128,128]{2,1,0:T(8,128)S(1)}, f32[5,224,128]{2,1,0:T(8,128)S(1)}, f32[128,128]{1,0:T(8,128)S(1)}, f32[8,128]{1,0:T(8,128)S(1)}, f32[5,5,8,1...) custom-call(f32[5,128,128]{2,1,0:T(8,128)} %bitcast.6, ...), custom_call_target="tpu_custom_call" | custom-call | tf_op jit(solution)/shard_map/exchange/pallas_call | solution.py:645
  12.4 0.9 %update.1 = (f32[5,8,16,128]{3,2,1,0:T(8,128)}, f32[5,8,16,128]{3,2,1,0:T(8,128)}) custom-call(f32[5,128,128]{2,1,0:T(8,128)S(1)} %get-tuple-element.11.acc, f32[5,224,128]{2,1,0:T(8,128)S(1)} %get-tuple-element.12.xpad, f32[128,128]{1,0:T(8,128)S(1)} %get-tuple-element.13.mask, f32[8,128]{1,0:T(8,128)S(1)} %get-tuple-element.14.first_alpha, ...), custom_call_target="tpu_custom_call" | custom-call | tf_op jit(solution)/shard_map/update/pallas_call | solution.py:690

commit v7 on v6

--- a/solution.py
+++ b/solution.py
@@ -304,20 +304,25 @@
     halo = 3 * ny
     strip = zt.shape[1] - 16
     chunk = strip // 8
-    load = pltpu.make_async_copy(state_ref, xpad.at[:, pl.ds(halo, rows), :], load_sem)
-    load.start()
+    half = rows // 2
+    loads = [
+        pltpu.make_async_copy(
+            state_ref.at[:, pl.ds(first, half), :], xpad.at[:, pl.ds(halo + first, half), :], load_sem.at[k]
+        )
+        for k, first in enumerate((0, half))
+    ]
+    for load in loads:
+        load.start()
     load_flags = pltpu.make_async_copy(flags_ref, flags, side_sem.at[0])
     load_ghost = pltpu.make_async_copy(ghost_ref, ghost, side_sem.at[1])
-    load_register = pltpu.make_async_copy(register_ref, reg, load_sem)
+    load_register = pltpu.make_async_copy(register_ref, reg, load_sem.at[0])
     slots[...] = jnp.zeros(slots.shape, slots.dtype)
     barrier = pltpu.get_barrier_semaphore()
     peers.greet(barrier)
-    load.wait()
-    load_flags.start()
-    load_ghost.start()
-    load_register.start()
     best = None
     for row in range(0, rows, 8):
+        if row % half == 0:
+            loads[row // half].wait()
         cons = [xpad[var, pl.ds(halo + row, 8), :] for var in range(5)]
         inverse, vel, pressure = pressure_velocity(cons)
         sound = jnp.sqrt(GAMMA * pressure * inverse)
@@ -325,6 +330,9 @@
         best = local if best is None else [jnp.maximum(a, b) for a, b in zip(best, local)]
     tops = [jnp.max(jnp.max(b, axis=0, keepdims=True), axis=1, keepdims=True) for b in best]
     lane = lax.broadcasted_iota(jnp.int32, (1, 128), 1)
+    load_flags.start()
+    load_ghost.start()
+    load_register.start()
     mine[...] = jnp.where(lane == 0, tops[0], jnp.where(lane == 1, tops[1], tops[2]))
 
     right, left = shifted(gx, 1, ngx), shifted(gx, ngx - 1, ngx)
@@ -674,7 +682,7 @@
             pltpu.VMEM((11, 5, cz // 8 + 4, 8, rows), f32),
             pltpu.VMEM((parts, 5, cx + 6, 8, cz), f32),
             pltpu.VMEM((parts, 11, 5, cx + 1, 8, cz), f32),
-            pltpu.SemaphoreType.DMA,
+            pltpu.SemaphoreType.DMA((2,)),
             pltpu.SemaphoreType.DMA((2,)),
             pltpu.SemaphoreType.DMA,
             pltpu.SemaphoreType.DMA((2,)),

time: 13.4 us -> 13.4 us (level)
  no operation moved by 1% of the time
where the time goes in v7:
time: 13.4 us; the launch traced here: 13.2 us
  Pallas kernels  12.6 us (94%)
  between operations  0.64 us (5%)
    pallas_call x1, Pallas kernels, shards(): pl.pallas_call(functools.partial(exchange_kernel, ngx, ngz, cx, ny), out_...  11.7 us
    pallas_call x1, Pallas kernels, shards(): pl.pallas_call(functools.partial(update_kernel, cx, ny), out_shape=(block...  0.87 us

profile of v7, /device:TPU:0, one launch (start us, length us, event | category | flops | bytes accessed | tf_op | source)
XLA Modules:
  0.0 13.2 jit_solution(9218104205406515409)
XLA Ops:
  0.6 11.7 %exchange.1 = (f32[5,128,128]{2,1,0:T(8,128)S(1)}, f32[5,224,128]{2,1,0:T(8,128)S(1)}, f32[128,128]{1,0:T(8,128)S(1)}, f32[8,128]{1,0:T(8,128)S(1)}, f32[5,5,8,1...) custom-call(f32[5,128,128]{2,1,0:T(8,128)} %bitcast.6, ...), custom_call_target="tpu_custom_call" | custom-call | tf_op jit(solution)/shard_map/exchange/pallas_call | solution.py:653
  12.4 0.9 %update.1 = (f32[5,8,16,128]{3,2,1,0:T(8,128)}, f32[5,8,16,128]{3,2,1,0:T(8,128)}) custom-call(f32[5,128,128]{2,1,0:T(8,128)S(1)} %get-tuple-element.11.acc, f32[5,224,128]{2,1,0:T(8,128)S(1)} %get-tuple-element.12.xpad, f32[128,128]{1,0:T(8,128)S(1)} %get-tuple-element.13.mask, f32[8,128]{1,0:T(8,128)S(1)} %get-tuple-element.14.first_alpha, ...), custom_call_target="tpu_custom_call" | custom-call | tf_op jit(solution)/shard_map/update/pallas_call | solution.py:698
